TPU v7x, 32 devices: a whole 2x2x4 slice. The times are simulated.
32 devices in a mesh: members: 2 (over y), comp: 4 (over z), lat: 2 (over x), sub: 2 (over core).
Axes of the slice: x: 2, y: 2, z: 4, core: 2. Of those that a mesh axis runs over, the one named last changes fastest.
Arguments:
- spectrum: float32 [1920, 4096], P('comp', ('members', 'lat', 'sub')), parts along dimension 1, may hold values from 0.05 to 2
- sea_mask: int32 [4096], P(('members', 'lat', 'sub')), parts along dimension 0, may hold values 0 or 1
- neighbours: int32 [4, 4096], P(None, ('members', 'lat', 'sub')), parts along dimension 1, may hold values from 0 to 2047, as said below
- substeps: int32 [30], replicated, may hold values from 1 to 6, as said below
- courant: float32 [30], replicated, may hold values from 0.2 to 0.7
- source_operator: bfloat16 [1920, 1920], P('sub'), may hold values from -0.125 to 0.125
Outputs:
- new_spectrum: float32 [1920, 4096], P('comp', ('members', 'lat', 'sub')), parts along dimension 1
There are 2 independent parts, one for each index of `members`. A program takes and returns all parts, laid end to end along the dimension named above; an argument that names none is the same for every part. Nothing has to cross between parts.
Inputs may be any that keep to these rules, and one draw needn't show every extreme that they name: Non-increasing with the band; the first band takes 6 substeps and the last band one. Points are numbered row by row, 256 to a row. The west and east neighbours lie in the same row, one or two columns away, wrapping around the row. The south neighbour lies in the row before and the north neighbour in the row after, within one column (wrapping); on the first and last row of the member's grid that neighbour is the point itself.
All inputs are finite; a program needn't handle non-finite values. No bound on the sum of `sea_mask` on one device may be relied on, other than what follows from the above.
Results may differ from a plain program's by a relative error of at most 0.0015.
Values may be sent and summed in bfloat16 or wider, within the bound.
A program may use at most 64 MiB of HBM per device.

v0:
```python
import functools
import math

import jax
import jax.numpy as jnp
import numpy as np
from jax import lax
from jax.experimental import pallas as pl
from jax.experimental.pallas import tpu as pltpu
from jax.sharding import PartitionSpec as P

NF = 30
ND = 64
NLON = 256
MAXSTEPS = 6
SRC_STEPS = 4
STEP_SIZE = 0.1
MESH = pl.DeviceIdType.MESH
HALF = ND // 2
TILES = 4
SLOTS = 8
F32 = jnp.float32
BF16 = jnp.bfloat16


def kernel(
    nlat, ncomp, group, spec_ref, mask_ref, nb_ref, steps_ref, cour_ref, cos_ref, sin_ref, op_ref,
    out_ref, w_ref, own_ref, halo_ref, code_ref, prop_ref, away_ref, got_ref, start_ref, state_ref,
    low_ref, inc_ref, home_ref,
    h_send, h_recv, w_send, w_recv, w_local, a_send, a_recv, b_send, b_recv,
):
    lat = lax.axis_index("lat")
    sub = lax.axis_index("sub")
    me = lax.axis_index("comp")
    bins, points = spec_ref.shape
    chunks, size = prop_ref.shape[0], prop_ref.shape[1]
    planes = size // 8
    share = points // ncomp
    total = bins * ncomp
    half_rows = total // 2
    first = me * bins
    last_lat = nlat - 1
    partner = {"sub": 1 - sub}

    barrier = pltpu.get_barrier_semaphore()
    peers = [partner]
    if nlat == 2:
        peers.append({"lat": 1 - lat})
    else:
        for move in (1, -1):
            peers.append({"lat": lax.rem(lat + move + nlat, nlat)})
            peers.append({"lat": lax.rem(lat + 2 * move + nlat, nlat), "sub": 1 - sub})
    for j in range(1, ncomp):
        peers.append({"comp": lax.rem(me + j, ncomp)})
    for peer in peers:
        pl.semaphore_signal(barrier, inc=1, device_id=peer, device_id_type=MESH)

    own_half = pl.ds(pl.multiple_of(sub * half_rows, 16), half_rows)
    load_w = pltpu.make_async_copy(op_ref, w_ref.at[own_half], w_local)
    load_w.start()

    lane = lax.broadcasted_iota(jnp.int32, (1, points), 1)
    column = lane & (NLON - 1)
    position = (lat * 2 + sub) * points + lane
    sea = mask_ref[...].astype(F32)
    west = (column - nb_ref[0:1, :]) & (NLON - 1)
    east = (nb_ref[1:2, :] - column) & (NLON - 1)

    def vertical(index_row):
        moved = ((index_row - column + 1) & (NLON - 1)) - 1
        return jnp.where(index_row == position, 2, moved)

    rows = lax.broadcasted_iota(jnp.int32, (size, points), 0)
    codes = jnp.zeros((size, points), F32)
    entries = [west, east, vertical(nb_ref[2:3, :]), vertical(nb_ref[3:4, :])]
    for k, entry in enumerate([e.astype(F32) for e in entries] + [sea]):
        codes = jnp.where(rows == k, jnp.broadcast_to(entry, (size, points)), codes)
    own_ref[0] = codes.astype(BF16)
    own_ref[1] = codes.astype(BF16)

    pl.semaphore_wait(barrier, len(peers))

    def kind(q):
        return lax.rem(lax.div(first + (q - 2) * size, HALF), 2)

    def has_from(ty, far):
        return jnp.where(ty == 0, lat >= far, lat <= last_lat - far)

    def has_to(ty, far):
        return jnp.where(ty == 0, lat <= last_lat - far, lat >= far)

    def pair_copy(q):
        return pltpu.make_async_remote_copy(
            src_ref=own_ref.at[q], dst_ref=halo_ref.at[0, q], send_sem=h_send.at[0, q],
            recv_sem=h_recv.at[0, q], device_id=partner, device_id_type=MESH)

    def side_copy(q, ty):
        to = jnp.clip(lat + 1 - 2 * ty, 0, last_lat)
        return pltpu.make_async_remote_copy(
            src_ref=own_ref.at[q], dst_ref=halo_ref.at[1, q], send_sem=h_send.at[1, q],
            recv_sem=h_recv.at[1, q], device_id={"lat": to}, device_id_type=MESH)

    def hand_copy(q, ty):
        slot = jnp.where(sub == ty, 2, 0)
        return pltpu.make_async_remote_copy(
            src_ref=halo_ref.at[1, q], dst_ref=halo_ref.at[slot, q], send_sem=h_send.at[2, q],
            recv_sem=h_recv.at[2, q], device_id=partner, device_id_type=MESH)

    def far_copy(q, ty):
        to = jnp.clip(lat + 2 - 4 * ty, 0, last_lat)
        return pltpu.make_async_remote_copy(
            src_ref=own_ref.at[q], dst_ref=halo_ref.at[2, q], send_sem=h_send.at[3, q],
            recv_sem=h_recv.at[3, q], device_id={"lat": to, "sub": 1 - sub}, device_id_type=MESH)

    def send_own(q, ty):
        @pl.when(has_to(ty, 1))
        def _():
            side_copy(q, ty).start()

        @pl.when(sub == ty)
        def _():
            pair_copy(q).start()

        if nlat > 2:
            @pl.when((sub != ty) & has_to(ty, 2))
            def _():
                far_copy(q, ty).start()

    def hand_on(q, ty):
        @pl.when(has_from(ty, 1))
        def _():
            side_copy(q, ty).wait_recv()
            hand_copy(q, ty).start()

    def arrive(q, ty):
        @pl.when(has_from(ty, 1))
        def _():
            hand_copy(q, ty).wait_recv()

        @pl.when(sub != ty)
        def _():
            pair_copy(q).wait_recv()

        if nlat > 2:
            @pl.when((sub == ty) & has_from(ty, 2))
            def _():
                far_copy(q, ty).wait_recv()

    def sent(q, ty):
        @pl.when(has_to(ty, 1))
        def _():
            side_copy(q, ty).wait_send()

        @pl.when(sub == ty)
        def _():
            pair_copy(q).wait_send()

        if nlat > 2:
            @pl.when((sub != ty) & has_to(ty, 2))
            def _():
                far_copy(q, ty).wait_send()

        @pl.when(has_from(ty, 1))
        def _():
            hand_copy(q, ty).wait_send()

    send_own(0, 0)
    send_own(1, 1)

    def prepare(i, carry):
        chunk = sea * spec_ref[pl.ds(pl.multiple_of(i * size, size), size), :]
        own_ref[i + 2] = chunk.astype(BF16)
        send_own(i + 2, kind(i + 2))
        return carry

    lax.fori_loop(0, chunks, prepare, 0)

    give_w = pltpu.make_async_remote_copy(
        src_ref=op_ref, dst_ref=w_ref.at[own_half], send_sem=w_send, recv_sem=w_recv,
        device_id=partner, device_id_type=MESH)
    give_w.start()

    for q in (0, 1):
        hand_on(q, q)
    ahead = min(6, chunks)
    for q in range(2, 2 + ahead):
        hand_on(q, kind(q))

    for ty in (0, 1):
        arrive(ty, ty)
        for slot in range(SLOTS):
            row = slot % 2 if ty == 0 else 1 - slot % 2
            cols = slice(row * NLON, (row + 1) * NLON)
            if slot < 6:
                part = halo_ref[2 - slot // 2, ty, :, cols].astype(F32)
            else:
                part = own_ref[ty, :, cols].astype(F32)
            for k, source in enumerate((0, 1, 2 + ty, 4)):
                code_ref[ty, slot, k] = jnp.broadcast_to(part[source:source + 1, :], (8, NLON))

    def propagate(i):
        q = i + 2
        ty = kind(q)

        @pl.when(i + ahead < chunks)
        def _():
            hand_on(q + ahead, kind(q + ahead))

        arrive(q, ty)
        bin0 = first + i * size
        freq = lax.div(bin0, ND)
        direction = lax.rem(bin0, ND)
        to_east = jnp.where((direction < ND // 4) | (direction >= 3 * ND // 4), 1, 0)
        steps = steps_ref[freq]
        speed = cour_ref[freq]
        sign = jnp.where(to_east == 1, 1.0, -1.0)
        shift1 = jnp.where(to_east == 1, 1, NLON - 1)
        shift2 = jnp.where(to_east == 1, 2, NLON - 2)
        back1 = NLON - shift1
        d8 = lax.div(direction, 8)
        abs_cos = cos_ref[pl.ds(d8, planes)]
        abs_sin = sin_ref[pl.ds(d8, planes)]

        def lanes(slot):
            row = jnp.where(ty == 0, slot % 2, 1 - slot % 2)
            return pl.ds(pl.multiple_of(row * NLON, NLON), NLON)

        values = []
        for slot in range(SLOTS):
            if slot < 6:
                part = halo_ref[2 - slot // 2, q, :, lanes(slot)].astype(F32)
            else:
                part = spec_ref[pl.ds(pl.multiple_of(i * size, size), size), lanes(slot)]
            part = part.reshape(planes, 8, NLON)
            if slot >= 6:
                part = part * code_ref[ty, slot, 3][None]
            values.append(part)
        for t in range(MAXSTEPS):
            live = jnp.where(t < steps, speed, 0.0)
            wx = live * abs_cos
            wy = live * abs_sin
            keep = 1.0 - wx - wy
            fresh = list(values)
            for slot in range(t + 1, SLOTS):
                x = values[slot]
                below = values[slot - 1]
                near = code_ref[ty, slot, 1 - to_east][None] == 1.0
                vert = code_ref[ty, slot, 2][None] * sign
                lon = jnp.where(near, pltpu.roll(x, shift1, 2), pltpu.roll(x, shift2, 2))
                up = jnp.where(vert == -1.0, pltpu.roll(below, shift1, 2),
                               jnp.where(vert == 1.0, pltpu.roll(below, back1, 2), below))
                up = jnp.where(jnp.abs(vert) == 2.0, x, up)
                fresh[slot] = code_ref[ty, slot, 3][None] * (keep * x + wx * lon + wy * up)
            values = fresh
        for slot in (6, 7):
            prop_ref[i, :, lanes(slot)] = values[slot].reshape(size, NLON)
        whole = prop_ref[i]
        for c in range(ncomp):
            away_ref[c, i] = whole[:, c * share:(c + 1) * share].astype(BF16)

    groups = chunks // group

    def out_copy(j, g):
        to = lax.rem(me + j, ncomp)
        span = pl.ds(g * group, group)
        return pltpu.make_async_remote_copy(
            src_ref=away_ref.at[to, span], dst_ref=got_ref.at[me, span],
            send_sem=a_send.at[j], recv_sem=a_recv.at[j],
            device_id={"comp": to}, device_id_type=MESH)

    def whole_copy(j):
        to = lax.rem(me + j, ncomp)
        return pltpu.make_async_remote_copy(
            src_ref=away_ref.at[to], dst_ref=got_ref.at[me],
            send_sem=a_send.at[j], recv_sem=a_recv.at[j],
            device_id={"comp": to}, device_id_type=MESH)

    def run_group(g, carry):
        def one(i, inner):
            propagate(g * group + i)
            return inner

        lax.fori_loop(0, group, one, 0)
        for j in range(1, ncomp):
            out_copy(j, g).start()
        return carry

    lax.fori_loop(0, groups, run_group, 0)

    for q in (0, 1):
        sent(q, q)

    def drain(q, carry):
        sent(q, kind(q))
        return carry

    lax.fori_loop(2, chunks + 2, drain, 0)
    got_ref[me] = away_ref[me]
    load_w.wait()
    give_w.wait()

    for j in range(1, ncomp):
        whole_copy(j).wait()
    for c in range(ncomp):
        start_ref[c * bins:(c + 1) * bins, :] = got_ref[c].astype(F32).reshape(bins, share)
    tile = total // TILES
    per_tile = bins // tile if bins >= tile else tile // bins
    for m in range(TILES):
        span = slice(m * tile, (m + 1) * tile)
        low_ref[0, span, :] = start_ref[span, :].astype(BF16)

    def tile_rows(m):
        return pl.ds(pl.multiple_of(m * tile, 16), tile)

    def advance(step, m):
        span = tile_rows(m)
        driving = jnp.dot(w_ref[span, :], low_ref[step % 2], preferred_element_type=F32)
        now = start_ref[span, :] if step == 0 else state_ref[span, :]
        return span, now + STEP_SIZE * now * driving

    for step in range(SRC_STEPS - 1):
        def one_tile(m, carry, step=step):
            span, now = advance(step, m)
            state_ref[span, :] = now
            low_ref[(step + 1) % 2, span, :] = now.astype(BF16)
            return carry

        lax.fori_loop(0, TILES, one_tile, 0)

    def home_copy(j, to):
        return pltpu.make_async_remote_copy(
            src_ref=inc_ref.at[to], dst_ref=home_ref.at[me],
            send_sem=b_send.at[j], recv_sem=b_recv.at[j],
            device_id={"comp": to}, device_id_type=MESH)

    mine = lax.div(me * TILES, ncomp)

    def last_tile(i, carry):
        m = lax.rem(mine + 1 + i, TILES)
        span, now = advance(SRC_STEPS - 1, m)
        gain = now - start_ref[span, :]
        for k in range(per_tile):
            to = m * per_tile + k
            inc_ref[to] = gain[k * bins:(k + 1) * bins, :].astype(BF16)
            j = lax.rem(to - me + ncomp, ncomp)

            @pl.when(to != me)
            def _():
                home_copy(j, to).start()

        return carry

    lax.fori_loop(0, TILES, last_tile, 0)
    home_ref[me] = inc_ref[me]
    for c in range(ncomp):
        j = lax.rem(me - c + ncomp, ncomp)

        @pl.when(me != c)
        def _():
            home_copy(j, lax.rem(me + j, ncomp)).wait()

        cols = slice(c * share, (c + 1) * share)
        before = prop_ref[:, :, cols].reshape(bins, share)
        out_ref[:, cols] = sea[:, cols] * (before + home_ref[c].astype(F32))


def solution(mesh):
    nlat, ncomp = mesh.shape["lat"], mesh.shape["comp"]

    def per_device(spectrum, sea_mask, neighbours, substeps, courant, source_operator):
        bins, points = spectrum.shape
        size = 16 if bins % 16 == 0 else 8
        chunks = bins // size
        group = 5 if chunks % 5 == 0 else 1
        share = points // ncomp
        total = bins * ncomp
        angles = (np.arange(ND, dtype=np.float32) + np.float32(0.5)) * np.float32(2.0 * math.pi / ND)
        spread = lambda v: jnp.asarray(
            np.broadcast_to(np.abs(v).astype(np.float32)[:, None], (ND, NLON)).reshape(ND // 8, 8, NLON))
        vmem = pl.BlockSpec(memory_space=pltpu.VMEM)
        smem = pl.BlockSpec(memory_space=pltpu.SMEM)
        kinds = 3 if nlat == 2 else 4
        return pl.pallas_call(
            functools.partial(kernel, nlat, ncomp, group),
            out_shape=jax.ShapeDtypeStruct((bins, points), F32),
            in_specs=[vmem, vmem, vmem, smem, smem, vmem, vmem, pl.BlockSpec(memory_space=pl.ANY)],
            out_specs=vmem,
            scratch_shapes=[
                pltpu.VMEM((total, total), BF16),
                pltpu.VMEM((chunks + 2, size, points), BF16),
                pltpu.VMEM((3, chunks + 2, size, points), BF16),
                pltpu.VMEM((2, SLOTS, 4, 8, NLON), F32),
                pltpu.VMEM((chunks, size, points), F32),
                pltpu.VMEM((ncomp, chunks, size, share), BF16),
                pltpu.VMEM((ncomp, chunks, size, share), BF16),
                pltpu.VMEM((total, share), F32),
                pltpu.VMEM((total, share), F32),
                pltpu.VMEM((2, total, share), BF16),
                pltpu.VMEM((ncomp, bins, share), BF16),
                pltpu.VMEM((ncomp, bins, share), BF16),
                pltpu.SemaphoreType.DMA((kinds, chunks + 2)),
                pltpu.SemaphoreType.DMA((kinds, chunks + 2)),
                pltpu.SemaphoreType.DMA,
                pltpu.SemaphoreType.DMA,
                pltpu.SemaphoreType.DMA,
                pltpu.SemaphoreType.DMA((ncomp,)),
                pltpu.SemaphoreType.DMA((ncomp,)),
                pltpu.SemaphoreType.DMA((ncomp,)),
                pltpu.SemaphoreType.DMA((ncomp,)),
            ],
            compiler_params=pltpu.CompilerParams(
                collective_id=0, has_side_effects=True, vmem_limit_bytes=56 * 1024 * 1024),
        )(spectrum, sea_mask.reshape(1, points), neighbours, substeps, courant,
          spread(np.cos(angles)), spread(np.sin(angles)), source_operator)

    placed = (
        P("comp", ("members", "lat", "sub")),
        P(("members", "lat", "sub")),
        P(None, ("members", "lat", "sub")),
        P(),
        P(),
        P("sub", None),
    )
    return jax.shard_map(
        per_device,
        mesh=mesh,
        in_specs=placed,
        out_specs=P("comp", ("members", "lat", "sub")),
        check_vma=False,
    )
```

profile of v0, /device:TPU:0, one launch (start us, length us, event | category | flops | bytes accessed | tf_op | source)
XLA Modules:
  0.0 64.4 jit_solution(2125192857612470837)
XLA Ops:
  0.0 1.4 %jit_solution_.6.cos_ref = f32[8,8,256]{2,1,0:T(8,128)} broadcast(f32[8,8]{1,0:T(8,128)} %constant.4.clone), dimensions={0,1} | broadcast | bytes 65792 | tf_op jit(solution)
  1.4 1.4 %jit_solution_.7.sin_ref = f32[8,8,256]{2,1,0:T(8,128)} broadcast(f32[8,8]{1,0:T(8,128)} %constant.5.clone), dimensions={0,1} | broadcast | bytes 65792 | tf_op jit(solution)
  2.8 59.4 %shard_map.82 = f32[480,512]{1,0:T(8,128)} custom-call(f32[480,512]{1,0:T(8,128)} %spec_ref.1, s32[1,512]{1,0:T(1,128)} %bitcast.1, s32[4,512]{1,0:T(4,128)} %nb_ref.1, s32[30]{0:T(128)} %steps_ref.1, f32[30]{0:T(128)} %cour_ref.1, f32[8,8,256]{2,1,0:T(8,128)} %jit_solution_.6.cos_ref, f32[8,8,256]{2,1,0:T(8,128)} %jit_solution_.7.sin_ref, ...), custom_call_target="tpu_custom_call" | custom-call | tf_op jit(solution)/shard_map/pallas_call | solution.py:383
  62.2 2.2 %copy.10 = f32[480,512]{1,0:T(8,128)} copy(f32[480,512]{1,0:T(8,128)} %shard_map.82) | data formatting | bytes 1966080
where the time goes:
time: 64.6 us; the launch traced here: 64.4 us
  Pallas kernels  59.4 us (92%)
  local copies, waits for them, and re-layouts  4.99 us (8%)
    pallas_call x1, Pallas kernels, per_device(): pl.pallas_call(functools.partial(kernel, nlat, ncomp, group), out_shape=j...  59.4 us
    another operation x2, local copies, waits for them, and re-layouts  2.78 us
    unnamed x1, local copies, waits for them, and re-layouts  2.21 us

commit v1 on v0

--- a/solution.py
+++ b/solution.py
@@ -19,6 +19,8 @@
 HALF = ND // 2
 TILES = 4
 SLOTS = 8
+NEAR = 4
+FAR = 2
 F32 = jnp.float32
 BF16 = jnp.bfloat16
 
@@ -364,11 +366,553 @@
         out_ref[:, cols] = sea[:, cols] * (before + home_ref[c].astype(F32))
 
 
+def fast_kernel(
+    ncomp, spec_ref, mask_ref, nb_ref, steps_ref, cour_ref, op_ref,
+    out_ref, w_ref, full_ref, oth_ref, hsend_ref, halo_ref, raw_ref, code_ref, ang_ref, perm_ref,
+    pout_ref, pin_ref, away_ref, x_ref, state_ref, inc_ref, home_ref,
+    l_sem, w_sem, c_send, c_recv, r_send, r_recv, h_send, h_recv, a_send, a_recv, o_sem,
+    f_send, f_recv, p_send, p_recv, e_send, e_recv, b_send, b_recv,
+):
+    lat = lax.axis_index("lat")
+    sub = lax.axis_index("sub")
+    me = lax.axis_index("comp")
+    groups = spec_ref.shape[0]
+    bins = groups * 2 * 16
+    kmax = halo_ref.shape[0]
+    lanes = NLON // 2
+    total = bins * ncomp
+    tiles = ncomp // 2
+    partner = {"sub": 1 - sub}
+    others = [partner, {"lat": 1 - lat}, {"lat": 1 - lat, "sub": 1 - sub}]
+
+    loads = []
+    for r in range(2):
+        cols = slice(r * NLON, (r + 1) * NLON)
+        loads.append(pltpu.make_async_copy(
+            spec_ref.at[:, 1 - sub, :, cols], oth_ref.at[pl.ds(0, groups), r], l_sem.at[r]))
+        loads.append(pltpu.make_async_copy(
+            spec_ref.at[:, sub, :, cols], full_ref.at[pl.ds(0, groups), 2 * sub + r], l_sem.at[2 + r]))
+    for load in (loads[0], loads[2], loads[1], loads[3]):
+        load.start()
+    load_w = pltpu.make_async_copy(op_ref, w_ref, w_sem)
+
+    barrier = pltpu.get_barrier_semaphore()
+    peers = list(others)
+    for d in range(1, ncomp):
+        z = lax.rem(me + d, ncomp)
+        peers += [{"comp": z}, {"comp": z, "sub": 1 - sub}]
+    for peer in peers:
+        pl.semaphore_signal(barrier, inc=1, device_id=peer, device_id_type=MESH)
+    load_w.start()
+
+    points = mask_ref.shape[1]
+    lane = lax.broadcasted_iota(jnp.int32, (1, points), 1)
+    column = lane & (NLON - 1)
+    sea = mask_ref[...].astype(F32)
+    west = (column - nb_ref[0:1, :]) & (NLON - 1)
+    east = (nb_ref[1:2, :] - column) & (NLON - 1)
+    moves = [((nb_ref[k:k + 1, :] - column + 1) & (NLON - 1)) - 1 for k in (2, 3)]
+    index = lax.broadcasted_iota(jnp.int32, (8, points), 0)
+    codes = jnp.zeros((8, points), F32)
+    for k, entry in enumerate([e.astype(F32) for e in (west, east, *moves)] + [sea]):
+        codes = jnp.where(index == k, jnp.broadcast_to(entry, (8, points)), codes)
+    raw_ref[lat, sub] = codes
+
+    a = lax.broadcasted_iota(jnp.int32, (NLON, NLON), 0)
+    b = lax.broadcasted_iota(jnp.int32, (NLON, NLON), 1)
+    split = lambda c: jnp.where(c < lanes, 2 * c, 2 * (c - lanes) + 1)
+    perm_ref[0] = (a == split(b)).astype(F32).astype(BF16)
+    perm_ref[1] = (b == split(a)).astype(F32).astype(BF16)
+
+    near_ty = lat
+    far_ty = 1 - lat
+    n0 = lax.rem(lat + me * groups, 2)
+    f0 = 1 - n0
+    for q, ty in enumerate((near_ty, far_ty)):
+        d = lax.broadcasted_iota(jnp.int32, (16, lanes), 0) + 16 * (2 * ty + sub)
+        angle = (d.astype(F32) + 0.5) * np.float32(2.0 * math.pi / ND)
+        ang_ref[q, 0] = jnp.abs(jnp.cos(angle))
+        ang_ref[q, 1] = jnp.abs(jnp.sin(angle))
+
+    for load in loads:
+        load.wait()
+    sea_rows = [jnp.broadcast_to(sea[:, r * NLON:(r + 1) * NLON], (16, NLON)) for r in range(2)]
+
+    def convert(k, carry):
+        j = n0 + 2 * k
+        for r in range(2):
+            mine = full_ref[j, 2 * sub + r] * sea_rows[r]
+            other = oth_ref[j, r] * sea_rows[r]
+            hsend_ref[k, sub, r] = mine.astype(BF16)
+            hsend_ref[k, 1 - sub, r] = other.astype(BF16)
+        return carry
+
+    lax.fori_loop(0, kmax, convert, 0)
+    pl.semaphore_wait(barrier, len(peers))
+
+    def code_copy(n):
+        return pltpu.make_async_remote_copy(
+            src_ref=raw_ref.at[lat, sub], dst_ref=raw_ref.at[lat, sub], send_sem=c_send.at[n],
+            recv_sem=c_recv.at[n], device_id=others[n], device_id_type=MESH)
+
+    def raw_copy():
+        return pltpu.make_async_remote_copy(
+            src_ref=oth_ref.at[pl.ds(0, groups)],
+            dst_ref=full_ref.at[pl.ds(0, groups), pl.ds(2 * sub, 2)],
+            send_sem=r_send, recv_sem=r_recv, device_id=partner, device_id_type=MESH)
+
+    def halo_copy(k, p):
+        return pltpu.make_async_remote_copy(
+            src_ref=hsend_ref.at[k, p], dst_ref=halo_ref.at[k, pl.ds(2 * sub, 2)],
+            send_sem=h_send.at[k, p], recv_sem=h_recv.at[k, sub],
+            device_id={"lat": 1 - lat, "sub": p}, device_id_type=MESH)
+
+    def halo_wait(k, s):
+        pltpu.make_async_remote_copy(
+            src_ref=hsend_ref.at[k, s], dst_ref=halo_ref.at[k, pl.ds(2 * s, 2)],
+            send_sem=h_send.at[k, s], recv_sem=h_recv.at[k, s],
+            device_id={"lat": 1 - lat, "sub": s}, device_id_type=MESH).wait_recv()
+
+    code_copy(0).start()
+    raw_copy().start()
+    code_copy(1).start()
+    code_copy(2).start()
+
+    def send_halo(k, carry):
+        @pl.when(n0 + 2 * k < groups)
+        def _():
+            for p in range(2):
+                halo_copy(k, p).start()
+        return carry
+
+    lax.fori_loop(0, kmax, send_halo, 0)
+
+    def decode(chip):
+        for s in range(2):
+            for r in range(2):
+                part = raw_ref[chip, s, :, r * NLON:(r + 1) * NLON].astype(BF16)
+                both = jnp.dot(part, perm_ref[0], preferred_element_type=F32)
+                for k in range(5):
+                    code_ref[chip, 2 * s + r, k] = jnp.broadcast_to(both[k:k + 1, :], (8, NLON))
+
+    def chunk_copy(h, j, d):
+        to = lax.rem(me + d, ncomp)
+        return pltpu.make_async_remote_copy(
+            src_ref=away_ref.at[h, to, j], dst_ref=x_ref.at[h, 0, me * groups + j, sub],
+            send_sem=a_send.at[h, d], recv_sem=a_recv.at[h, me],
+            device_id={"comp": to}, device_id_type=MESH)
+
+    def whole_copy(h, d):
+        to = lax.rem(me + d, ncomp)
+        return pltpu.make_async_remote_copy(
+            src_ref=away_ref.at[h, to, pl.ds(0, groups)],
+            dst_ref=x_ref.at[h, 0, pl.ds(me * groups, groups), sub],
+            send_sem=a_send.at[h, d], recv_sem=a_recv.at[h, me],
+            device_id={"comp": to}, device_id_type=MESH)
+
+    def whole_wait(h, z):
+        pltpu.make_async_remote_copy(
+            src_ref=away_ref.at[h, z, pl.ds(0, groups)],
+            dst_ref=x_ref.at[h, 0, pl.ds(z * groups, groups), sub],
+            send_sem=a_send.at[h, 0], recv_sem=a_recv.at[h, z],
+            device_id={"comp": z}, device_id_type=MESH).wait_recv()
+
+    def pick(ty, i):
+        return ty * 3 + (1 - 2 * ty) * i
+
+    def separate(x):
+        high = x.astype(BF16)
+        low = (x - high.astype(F32)).astype(BF16)
+        return high, low
+
+    def propagate(ks, far, to_east):
+        ty = far_ty if far else near_ty
+        js = [(f0 if far else n0) + 2 * k for k in ks]
+        vert = 2 + ty
+        lowest = 0 if far else 4
+
+        def code(q, k, half):
+            chip = lat if q >= 4 else 1 - lat
+            part = code_ref[chip, pick(ty, q % 4), k, :, half * lanes:(half + 1) * lanes]
+            return jnp.concatenate([part, part], axis=0)
+
+        raw = jnp.concatenate([full_ref[j, pick(ty, i)] for j in js for i in range(4)], axis=0)
+        high, low = separate(raw)
+        mixed = (jnp.dot(high, perm_ref[0], preferred_element_type=F32)
+                 + jnp.dot(low, perm_ref[0], preferred_element_type=F32))
+        if far:
+            edge = jnp.concatenate([halo_ref[k, pick(ty, i)] for k in ks for i in range(4)], axis=0)
+            edge = jnp.dot(edge, perm_ref[0], preferred_element_type=F32)
+        cells = []
+        weights = []
+        for n, j in enumerate(js):
+            values = [None] * 8
+            for i in range(4):
+                rows = slice((n * 4 + i) * 16, (n * 4 + i + 1) * 16)
+                values[4 + i] = tuple(
+                    mixed[rows, half * lanes:(half + 1) * lanes] * code(4 + i, 4, half)
+                    for half in range(2))
+                if far:
+                    values[i] = tuple(edge[rows, half * lanes:(half + 1) * lanes] for half in range(2))
+            cells.append(values)
+            freq = jnp.minimum(lax.div(me * bins + j * 32, ND), steps_ref.shape[0] - 1)
+            weights.append((steps_ref[freq], cour_ref[freq]))
+        abs_cos, abs_sin = ang_ref[int(far), 0], ang_ref[int(far), 1]
+        ahead, behind = (1, lanes - 1)
+        for t in range(MAXSTEPS):
+            slots = [q for q in range(7, lowest - 1, -1) if q >= 4 or t <= q + 1]
+            for n, (steps, speed) in enumerate(weights):
+                live = jnp.where(t < steps, speed, 0.0)
+                wx = live * abs_cos
+                wy = live * abs_sin
+                keep = 1.0 - wx - wy
+                values = cells[n]
+                fresh = list(values)
+                turned = {}
+
+                def turn(q, half, shift):
+                    key = (q, half, shift)
+                    if key not in turned:
+                        turned[key] = pltpu.roll(values[q][half], shift, 1)
+                    return turned[key]
+
+                def left(q):
+                    return turn(q, 1, ahead), values[q][0]
+
+                def right(q):
+                    return values[q][1], turn(q, 0, behind)
+
+                for q in slots:
+                    shift = ahead if to_east else behind
+                    one = left(q) if to_east else right(q)
+                    lon_code = 0 if to_east else 1
+                    new = []
+                    for half in range(2):
+                        x = values[q][half]
+                        lon = jnp.where(code(q, lon_code, half) == 1.0, one[half], turn(q, half, shift))
+                        if q == lowest:
+                            up = x
+                        else:
+                            move = code(q, vert, half)
+                            up = jnp.where(move == -1.0, left(q - 1)[half],
+                                           jnp.where(move == 1.0, right(q - 1)[half], values[q - 1][half]))
+                        new.append(code(q, 4, half) * (keep * x + wx * lon + wy * up))
+                    fresh[q] = tuple(new)
+                cells[n] = fresh
+        for n, j in enumerate(js):
+            for i in range(4):
+                r = pick(ty, i)
+                for half in range(2):
+                    value = cells[n][4 + i][half]
+                    pout_ref[j, r, :, half * lanes:(half + 1) * lanes] = value
+                    away_ref[lax.div(r, 2), 2 * lax.rem(r, 2) + half, j] = value.astype(BF16)
+        for n, j in enumerate(js):
+            @pl.when(j < groups)
+            def _():
+                for d in range(1, ncomp):
+                    chunk_copy(0, j, d).start()
+
+    straight = sub == lat
+    code_copy(0).wait_recv()
+    decode(lat)
+    raw_copy().wait_recv()
+
+    def near_body(g, carry):
+        ks = [g * NEAR + n for n in range(NEAR)]
+
+        @pl.when(straight)
+        def _():
+            propagate(ks, False, True)
+
+        @pl.when(jnp.logical_not(straight))
+        def _():
+            propagate(ks, False, False)
+        return carry
+
+    lax.fori_loop(0, kmax // NEAR, near_body, 0)
+    code_copy(1).wait_recv()
+    code_copy(2).wait_recv()
+    decode(1 - lat)
+
+    def far_body(g, carry):
+        ks = [g * FAR + n for n in range(FAR)]
+        for k in ks:
+            @pl.when(f0 + 2 * k < groups)
+            def _():
+                for s in range(2):
+                    halo_wait(k, s)
+
+        @pl.when(straight)
+        def _():
+            propagate(ks, True, False)
+
+        @pl.when(jnp.logical_not(straight))
+        def _():
+            propagate(ks, True, True)
+        return carry
+
+    lax.fori_loop(0, kmax // FAR, far_body, 0)
+
+    def own_copy(h):
+        return pltpu.make_async_copy(
+            away_ref.at[h, me, pl.ds(0, groups)],
+            x_ref.at[h, 0, pl.ds(me * groups, groups), sub], o_sem.at[h])
+
+    def own_forward(h):
+        return pltpu.make_async_remote_copy(
+            src_ref=away_ref.at[h, me, pl.ds(0, groups)],
+            dst_ref=x_ref.at[h, 0, pl.ds(me * groups, groups), sub],
+            send_sem=f_send.at[h, 0], recv_sem=f_recv.at[h, 0],
+            device_id=partner, device_id_type=MESH)
+
+    def forward(h, d):
+        z = lax.rem(me + d, ncomp)
+        span = x_ref.at[h, 0, pl.ds(z * groups, groups), sub]
+        return pltpu.make_async_remote_copy(
+            src_ref=span, dst_ref=span, send_sem=f_send.at[h, d], recv_sem=f_recv.at[h, d],
+            device_id=partner, device_id_type=MESH)
+
+    def forward_wait(h, d):
+        z = lax.rem(me + d, ncomp)
+        span = x_ref.at[h, 0, pl.ds(z * groups, groups), 1 - sub]
+        pltpu.make_async_remote_copy(
+            src_ref=span, dst_ref=span, send_sem=f_send.at[h, d], recv_sem=f_recv.at[h, d],
+            device_id=partner, device_id_type=MESH).wait_recv()
+
+    def prop_copy():
+        return pltpu.make_async_remote_copy(
+            src_ref=pout_ref.at[pl.ds(0, groups), pl.ds(2 * (1 - sub), 2)],
+            dst_ref=pin_ref, send_sem=p_send, recv_sem=p_recv,
+            device_id=partner, device_id_type=MESH)
+
+    for d in range(1, ncomp):
+        whole_copy(1, d).start()
+    for h in range(2):
+        own_copy(h).start()
+        own_forward(h).start()
+    prop_copy().start()
+    load_w.wait()
+
+    def collect(h):
+        for d in range(1, ncomp):
+            whole_wait(h, lax.rem(me + d, ncomp))
+            forward(h, d).start()
+
+    def complete(h):
+        own_copy(h).wait()
+        for d in range(ncomp):
+            forward_wait(h, d)
+
+    first = sub * tiles * groups
+
+    def state_copy(h, step, m):
+        span = x_ref.at[h, step + 1, pl.ds(first + m * groups, groups)]
+        return pltpu.make_async_remote_copy(
+            src_ref=span, dst_ref=span, send_sem=e_send.at[h, step, m], recv_sem=e_recv.at[h, step, m],
+            device_id=partner, device_id_type=MESH)
+
+    def state_wait(h, step, m):
+        span = x_ref.at[h, step + 1, pl.ds((1 - sub) * tiles * groups + m * groups, groups)]
+        pltpu.make_async_remote_copy(
+            src_ref=span, dst_ref=span, send_sem=e_send.at[h, step, m], recv_sem=e_recv.at[h, step, m],
+            device_id=partner, device_id_type=MESH).wait_recv()
+
+    def home_copy(h, m):
+        to = sub * tiles + m
+        return to, pltpu.make_async_remote_copy(
+            src_ref=inc_ref.at[h, m], dst_ref=home_ref.at[me],
+            send_sem=b_send.at[h, m], recv_sem=b_recv.at[me],
+            device_id={"comp": to, "sub": h}, device_id_type=MESH)
+
+    def advance(h, step):
+        def one(i, carry):
+            m = lax.rem(i + 1 + me, tiles)
+            rows = pl.ds(pl.multiple_of(m * bins, 16), bins)
+            field = x_ref[h, step].reshape(total, lanes)
+            driving = jnp.dot(w_ref[rows, :], field, preferred_element_type=F32)
+            if step == 0:
+                now = x_ref[h, 0, pl.ds(first + m * groups, groups)].reshape(bins, lanes).astype(F32)
+            else:
+                now = state_ref[h, rows, :]
+            now = now + STEP_SIZE * now * driving
+            if step < SRC_STEPS - 1:
+                state_ref[h, rows, :] = now
+                x_ref[h, step + 1, pl.ds(first + m * groups, groups)] = now.astype(BF16).reshape(
+                    groups, 2, 16, lanes)
+                state_copy(h, step, m).start()
+            else:
+                start = x_ref[h, 0, pl.ds(first + m * groups, groups)].reshape(bins, lanes).astype(F32)
+                gain = (now - start).astype(BF16)
+                inc_ref[h, m] = gain
+                to, copy = home_copy(h, m)
+                local = (to == me) & (sub == h)
+
+                @pl.when(jnp.logical_not(local))
+                def _():
+                    copy.start()
+
+                @pl.when(local)
+                def _():
+                    home_ref[me] = inc_ref[h, m]
+            return carry
+
+        if step > 0:
+            for m in range(tiles):
+                state_wait(h, step - 1, m)
+        lax.fori_loop(0, tiles, one, 0)
+
+    collect(0)
+    complete(0)
+    advance(0, 0)
+    advance(0, 1)
+    advance(0, 2)
+    collect(1)
+    advance(0, 3)
+    complete(1)
+    for step in range(SRC_STEPS):
+        advance(1, step)
+
+    sea_wide = [jnp.broadcast_to(sea[:, r * NLON:(r + 1) * NLON], (16, NLON)) for r in range(2)]
+    prop_copy().wait_recv()
+
+    def restore(j, carry):
+        parts = [pout_ref[j, 2 * sub], pout_ref[j, 2 * sub + 1], pin_ref[j, 0], pin_ref[j, 1]]
+        high, low = separate(jnp.concatenate(parts, axis=0))
+        plain = (jnp.dot(high, perm_ref[1], preferred_element_type=F32)
+                 + jnp.dot(low, perm_ref[1], preferred_element_type=F32))
+        for n in range(4):
+            p = sub if n < 2 else 1 - sub
+            rows = pl.ds(pl.multiple_of((2 * j + p) * 16, 16), 16)
+            r = n % 2
+            out_ref[rows, r * NLON:(r + 1) * NLON] = sea_wide[r] * plain[n * 16:(n + 1) * 16, :]
+        return carry
+
+    lax.fori_loop(0, groups, restore, 0)
+
+    mine_local = lax.div(me, tiles) == sub
+    for d in (0, 1, 3, 2):
+        z = lax.rem(me + d, ncomp)
+
+        def land():
+            pltpu.make_async_remote_copy(
+                src_ref=inc_ref.at[0, 0], dst_ref=home_ref.at[z],
+                send_sem=b_send.at[0, 0], recv_sem=b_recv.at[z],
+                device_id={"comp": z}, device_id_type=MESH).wait_recv()
+
+        if d == 0:
+            pl.when(jnp.logical_not(mine_local))(land)
+        else:
+            land()
+        r = lax.div(z, 2)
+        half = lax.rem(z, 2)
+        cols = pl.ds(pl.multiple_of(r * NLON, NLON), NLON)
+        spread = perm_ref[1, pl.ds(pl.multiple_of(half * lanes, lanes), lanes), :]
+        sea_row = jnp.where(r == 0, sea_wide[0][0:8], sea_wide[1][0:8])
+        back = jnp.dot(home_ref[z], spread, preferred_element_type=F32)
+        back = back.reshape(bins // 8, 8, NLON) * sea_row[None]
+        out_ref[:, cols] = out_ref[:, cols] + back.reshape(bins, NLON)
+
+    for n in range(3):
+        code_copy(n).wait_send()
+    raw_copy().wait_send()
+
+    def halo_left(k, carry):
+        @pl.when(n0 + 2 * k < groups)
+        def _():
+            for p in range(2):
+                halo_copy(k, p).wait_send()
+        return carry
+
+    lax.fori_loop(0, kmax, halo_left, 0)
+    prop_copy().wait_send()
+    for h in range(2):
+        own_forward(h).wait_send()
+        for d in range(1, ncomp):
+            whole_copy(h, d).wait_send()
+            forward(h, d).wait_send()
+        for m in range(tiles):
+            for step in range(SRC_STEPS - 1):
+                state_copy(h, step, m).wait_send()
+            to, copy = home_copy(h, m)
+
+            @pl.when(jnp.logical_not((to == me) & (sub == h)))
+            def _():
+                copy.wait_send()
+
+
+def write_kernel(src_ref, dst_ref, sems):
+    pieces = sems.shape[0]
+    rows = src_ref.shape[0] // pieces
+    copies = [pltpu.make_async_copy(
+        src_ref.at[pl.ds(i * rows, rows)], dst_ref.at[pl.ds(i * rows, rows)], sems.at[i])
+        for i in range(pieces)]
+    for copy in copies:
+        copy.start()
+    for copy in copies:
+        copy.wait()
+
+
+def fast_device(ncomp, spectrum, sea_mask, neighbours, substeps, courant, source_operator):
+    bins, points = spectrum.shape
+    groups = bins // 32
+    kmax = (groups + 1) // 2
+    lanes = NLON // 2
+    total = bins * ncomp
+    tiles = ncomp // 2
+    vmem = pl.BlockSpec(memory_space=pltpu.VMEM)
+    smem = pl.BlockSpec(memory_space=pltpu.SMEM)
+    hbm = pl.BlockSpec(memory_space=pl.ANY)
+    dma = pltpu.SemaphoreType.DMA
+    result = pl.pallas_call(
+        functools.partial(fast_kernel, ncomp),
+        out_shape=pltpu.VMEM((bins, points), F32),
+        in_specs=[hbm, vmem, vmem, smem, smem, hbm],
+        out_specs=vmem,
+        scratch_shapes=[
+            pltpu.VMEM((total // 2, total), BF16),
+            pltpu.VMEM((2 * kmax, 4, 16, NLON), F32),
+            pltpu.VMEM((2 * kmax, 2, 16, NLON), F32),
+            pltpu.VMEM((kmax, 2, 2, 16, NLON), BF16),
+            pltpu.VMEM((kmax, 4, 16, NLON), BF16),
+            pltpu.VMEM((2, 2, 8, points), F32),
+            pltpu.VMEM((2, 4, 5, 8, NLON), F32),
+            pltpu.VMEM((2, 2, 16, lanes), F32),
+            pltpu.VMEM((2, NLON, NLON), BF16),
+            pltpu.VMEM((2 * kmax, 4, 16, NLON), F32),
+            pltpu.VMEM((groups, 2, 16, NLON), F32),
+            pltpu.VMEM((2, ncomp, 2 * kmax, 16, lanes), BF16),
+            pltpu.VMEM((2, SRC_STEPS, ncomp * groups, 2, 16, lanes), BF16),
+            pltpu.VMEM((2, total // 2, lanes), F32),
+            pltpu.VMEM((2, tiles, bins, lanes), BF16),
+            pltpu.VMEM((ncomp, bins, lanes), BF16),
+            dma((4,)), dma, dma((3,)), dma((3,)), dma, dma,
+            dma((kmax, 2)), dma((kmax, 2)), dma((2, ncomp)), dma((2, ncomp)), dma((2,)),
+            dma((2, ncomp)), dma((2, ncomp)), dma, dma,
+            dma((2, SRC_STEPS - 1, tiles)), dma((2, SRC_STEPS - 1, tiles)),
+            dma((2, tiles)), dma((ncomp,)),
+        ],
+        compiler_params=pltpu.CompilerParams(
+            collective_id=1, has_side_effects=True, vmem_limit_bytes=48 * 1024 * 1024),
+    )(spectrum.reshape(groups, 2, 16, points), sea_mask.reshape(1, points), neighbours, substeps, courant,
+      source_operator)
+    return pl.pallas_call(
+        write_kernel,
+        out_shape=jax.ShapeDtypeStruct((bins, points), F32),
+        in_specs=[vmem],
+        out_specs=hbm,
+        scratch_shapes=[dma((4,))],
+        compiler_params=pltpu.CompilerParams(vmem_limit_bytes=4 * 1024 * 1024),
+    )(result)
+
+
 def solution(mesh):
     nlat, ncomp = mesh.shape["lat"], mesh.shape["comp"]
 
     def per_device(spectrum, sea_mask, neighbours, substeps, courant, source_operator):
         bins, points = spectrum.shape
+        even = bins % 32 == 0 and (bins // 32 + 1) // 2 % NEAR == 0
+        if nlat == 2 and ncomp == 4 and points == 2 * NLON and even:
+            return fast_device(ncomp, spectrum, sea_mask, neighbours, substeps, courant, source_operator)
         size = 16 if bins % 16 == 0 else 8
         chunks = bins // size
         group = 5 if chunks % 5 == 0 else 1

time: 64.6 us -> 50.8 us (0.79)
  the two profiles are of different devices: /device:TPU:0 before, /device:TPU:1 now
where the time goes in v1:
time: 50.8 us; the launch traced here: 50.5 us
  Pallas kernels  44.5 us (88%)
  local copies, waits for them, and re-layouts  5.93 us (12%)
    pallas_call x1, Pallas kernels, fast_device(): pl.pallas_call(functools.partial(fast_kernel, ncomp), out_shape=pltpu.VME...  43.6 us
    unnamed x12, local copies, waits for them, and re-layouts  5.93 us

profile of v1, /device:TPU:1, one launch (start us, length us, event | category | flops | bytes accessed | tf_op | source)
XLA Modules:
  0.0 50.5 jit_solution(11562643465082246093)
XLA Ops:
  0.0 0.0 copy-start
  0.0 2.0 %copy-done = bf16[960,1920]{1,0:T(8,128)(2,1)S(1)} copy-done((bf16[960,1920]{1,0:T(8,128)(2,1)S(1)}, bf16[960,1920]{1,0:T(8,128)(2,1)}, u32[]{:S(2)}) %copy-start) | copy-done | bytes 3686424
  2.0 0.0 copy-start.1
  2.0 1.2 %copy-done.1 = f32[480,512]{1,0:T(8,128)S(1)} copy-done((f32[480,512]{1,0:T(8,128)S(1)}, f32[480,512]{1,0:T(8,128)}, u32[]{:S(2)}) %copy-start.1) | copy-done | bytes 983064
  3.2 0.0 copy-start.2
  3.2 0.7 %copy-done.2 = s32[4,512]{1,0:T(4,128)S(1)} copy-done((s32[4,512]{1,0:T(4,128)S(1)}, s32[4,512]{1,0:T(4,128)}, u32[]{:S(2)}) %copy-start.2) | copy-done | bytes 8216
  3.9 0.0 copy-start.3
  3.9 0.7 %copy-done.3 = s32[512]{0:T(512)S(1)} copy-done((s32[512]{0:T(512)S(1)}, s32[512]{0:T(512)}, u32[]{:S(2)}) %copy-start.3) | copy-done | bytes 2072
  4.6 0.0 copy-start.4
  4.6 0.7 %copy-done.4 = s32[30]{0:T(128)S(1)} copy-done((s32[30]{0:T(128)S(1)}, s32[30]{0:T(128)}, u32[]{:S(2)}) %copy-start.4) | copy-done | bytes 144
  5.3 0.0 copy-start.5
  5.3 0.7 %copy-done.5 = f32[30]{0:T(128)S(1)} copy-done((f32[30]{0:T(128)S(1)}, f32[30]{0:T(128)}, u32[]{:S(2)}) %copy-start.5) | copy-done | bytes 144
  5.9 43.6 %shard_map.64.src_ref = f32[480,512]{1,0:T(8,128)S(1)} custom-call(f32[15,2,16,512]{3,2,1,0:T(8,128)S(1)} %bitcast.2, s32[1,512]{1,0:T(1,128)S(1)} %bitcast.3, s32[4,512]{1,0:T(4,128)S(1)} %copy-done.2, s32[30]{0:T(128)S(1)} %copy-done.4, f32[30]{0:T(128)S(1)} %copy-done.5, bf16[960,1920]{1,0:T(8,128)(2,1)S(1)} %copy-done), custom_call_target="tpu_custom_call" | custom-call | tf_op jit(solution)/shard_map/pallas_call | solution.py:866
  49.5 1.0 %shard_map.65 = f32[480,512]{1,0:T(8,128)} custom-call(f32[480,512]{1,0:T(8,128)S(1)} %shard_map.64.src_ref), custom_call_target="tpu_custom_call" | custom-call | tf_op jit(solution)/shard_map/pallas_call | solution.py:898
Async XLA Ops:
  0.0 2.0 %copy-start = (bf16[960,1920]{1,0:T(8,128)(2,1)S(1)}, bf16[960,1920]{1,0:T(8,128)(2,1)}, u32[]{:S(2)}) copy-start(bf16[960,1920]{1,0:T(8,128)(2,1)} %op_ref.1) | copy-start | bytes 11059204
  2.0 1.2 %copy-start.1 = (f32[480,512]{1,0:T(8,128)S(1)}, f32[480,512]{1,0:T(8,128)}, u32[]{:S(2)}) copy-start(f32[480,512]{1,0:T(8,128)} %param.6) | copy-start | bytes 2949124
  3.2 0.7 %copy-start.2 = (s32[4,512]{1,0:T(4,128)S(1)}, s32[4,512]{1,0:T(4,128)}, u32[]{:S(2)}) copy-start(s32[4,512]{1,0:T(4,128)} %nb_ref.1) | copy-start | bytes 24580
  3.9 0.7 %copy-start.3 = (s32[512]{0:T(512)S(1)}, s32[512]{0:T(512)}, u32[]{:S(2)}) copy-start(s32[512]{0:T(512)} %param.7) | copy-start | bytes 6148
  4.6 0.7 %copy-start.4 = (s32[30]{0:T(128)S(1)}, s32[30]{0:T(128)}, u32[]{:S(2)}) copy-start(s32[30]{0:T(128)} %steps_ref.1) | copy-start | bytes 364
  5.3 0.7 %copy-start.5 = (f32[30]{0:T(128)S(1)}, f32[30]{0:T(128)}, u32[]{:S(2)}) copy-start(f32[30]{0:T(128)} %cour_ref.1) | copy-start | bytes 364

commit v2 on v1

--- a/solution.py
+++ b/solution.py
@@ -21,6 +21,7 @@
 SLOTS = 8
 NEAR = 4
 FAR = 2
+BACK = 5
 F32 = jnp.float32
 BF16 = jnp.bfloat16
 
@@ -367,11 +368,11 @@
 
 
 def fast_kernel(
-    ncomp, spec_ref, mask_ref, nb_ref, steps_ref, cour_ref, op_ref,
-    out_ref, w_ref, full_ref, oth_ref, hsend_ref, halo_ref, raw_ref, code_ref, ang_ref, perm_ref,
-    pout_ref, pin_ref, away_ref, x_ref, state_ref, inc_ref, home_ref,
-    l_sem, w_sem, c_send, c_recv, r_send, r_recv, h_send, h_recv, a_send, a_recv, o_sem,
-    f_send, f_recv, p_send, p_recv, e_send, e_recv, b_send, b_recv,
+    ncomp, spec_ref, mask_hbm, nb_hbm, steps_hbm, cour_hbm, op_ref,
+    out_ref, mask_ref, nb_ref, steps_ref, cour_ref, w_ref, full_ref, oth_ref, hsend_ref, halo_ref, raw_ref, code_ref, ang_ref, perm_ref,
+    pout_ref, pin_ref, away_ref, x_ref, start_ref, state_ref, inc_ref, home_ref,
+    l_sem, i_sem, w_sem, c_send, c_recv, r_send, r_recv, g_send, g_recv, h_send, h_recv,
+    a_send, a_recv, o_sem, p_send, p_recv, b_send, b_recv,
 ):
     lat = lax.axis_index("lat")
     sub = lax.axis_index("sub")
@@ -381,10 +382,13 @@
     kmax = halo_ref.shape[0]
     lanes = NLON // 2
     total = bins * ncomp
-    tiles = ncomp // 2
     partner = {"sub": 1 - sub}
     others = [partner, {"lat": 1 - lat}, {"lat": 1 - lat, "sub": 1 - sub}]
 
+    small = [pltpu.make_async_copy(src, dst, i_sem.at[n]) for n, (src, dst) in enumerate((
+        (mask_hbm, mask_ref), (nb_hbm, nb_ref), (steps_hbm, steps_ref), (cour_hbm, cour_ref)))]
+    for load in small:
+        load.start()
     loads = []
     for r in range(2):
         cols = slice(r * NLON, (r + 1) * NLON)
@@ -394,7 +398,8 @@
             spec_ref.at[:, sub, :, cols], full_ref.at[pl.ds(0, groups), 2 * sub + r], l_sem.at[2 + r]))
     for load in (loads[0], loads[2], loads[1], loads[3]):
         load.start()
-    load_w = pltpu.make_async_copy(op_ref, w_ref, w_sem)
+    own_half = pl.ds(pl.multiple_of(sub * (total // 2), 16), total // 2)
+    load_w = pltpu.make_async_copy(op_ref, w_ref.at[own_half], w_sem)
 
     barrier = pltpu.get_barrier_semaphore()
     peers = list(others)
@@ -404,6 +409,8 @@
     for peer in peers:
         pl.semaphore_signal(barrier, inc=1, device_id=peer, device_id_type=MESH)
     load_w.start()
+    for load in small:
+        load.wait()
 
     points = mask_ref.shape[1]
     lane = lax.broadcasted_iota(jnp.int32, (1, points), 1)
@@ -478,6 +485,17 @@
     code_copy(1).start()
     code_copy(2).start()
 
+    def give_w():
+        return pltpu.make_async_remote_copy(
+            src_ref=op_ref, dst_ref=w_ref.at[own_half], send_sem=g_send, recv_sem=g_recv,
+            device_id=partner, device_id_type=MESH)
+
+    def take_w():
+        other_half = pl.ds(pl.multiple_of((1 - sub) * (total // 2), 16), total // 2)
+        return pltpu.make_async_remote_copy(
+            src_ref=op_ref, dst_ref=w_ref.at[other_half], send_sem=g_send, recv_sem=g_recv,
+            device_id=partner, device_id_type=MESH)
+
     def send_halo(k, carry):
         @pl.when(n0 + 2 * k < groups)
         def _():
@@ -486,6 +504,7 @@
         return carry
 
     lax.fori_loop(0, kmax, send_halo, 0)
+    give_w().start()
 
     def decode(chip):
         for s in range(2):
@@ -495,27 +514,33 @@
                 for k in range(5):
                     code_ref[chip, 2 * s + r, k] = jnp.broadcast_to(both[k:k + 1, :], (8, NLON))
 
-    def chunk_copy(h, j, d):
-        to = lax.rem(me + d, ncomp)
-        return pltpu.make_async_remote_copy(
-            src_ref=away_ref.at[h, to, j], dst_ref=x_ref.at[h, 0, me * groups + j, sub],
-            send_sem=a_send.at[h, d], recv_sem=a_recv.at[h, me],
-            device_id={"comp": to}, device_id_type=MESH)
-
-    def whole_copy(h, d):
-        to = lax.rem(me + d, ncomp)
+    side = lax.div(me, 2)
+
+    def target(i):
+        near = me + 1 - 2 * lax.rem(me, 2)
+        return jnp.where(i == 0, 3 - 3 * side, jnp.where(i == 1, 2 - side, jnp.where(i == 2, near, me)))
+
+    def chunk_copy(h, j, i):
+        to = target(i)
+        return pltpu.make_async_remote_copy(
+            src_ref=away_ref.at[h, to, j], dst_ref=x_ref.at[0, me * groups + j, sub],
+            send_sem=a_send.at[h, i], recv_sem=a_recv.at[me, sub],
+            device_id={"comp": to, "sub": h}, device_id_type=MESH)
+
+    def whole_copy(h, i):
+        to = target(i)
         return pltpu.make_async_remote_copy(
             src_ref=away_ref.at[h, to, pl.ds(0, groups)],
-            dst_ref=x_ref.at[h, 0, pl.ds(me * groups, groups), sub],
-            send_sem=a_send.at[h, d], recv_sem=a_recv.at[h, me],
-            device_id={"comp": to}, device_id_type=MESH)
-
-    def whole_wait(h, z):
+            dst_ref=x_ref.at[0, pl.ds(me * groups, groups), sub],
+            send_sem=a_send.at[h, i], recv_sem=a_recv.at[me, sub],
+            device_id={"comp": to, "sub": h}, device_id_type=MESH)
+
+    def whole_wait(z, s):
         pltpu.make_async_remote_copy(
-            src_ref=away_ref.at[h, z, pl.ds(0, groups)],
-            dst_ref=x_ref.at[h, 0, pl.ds(z * groups, groups), sub],
-            send_sem=a_send.at[h, 0], recv_sem=a_recv.at[h, z],
-            device_id={"comp": z}, device_id_type=MESH).wait_recv()
+            src_ref=away_ref.at[0, z, pl.ds(0, groups)],
+            dst_ref=x_ref.at[0, pl.ds(z * groups, groups), s],
+            send_sem=a_send.at[0, 0], recv_sem=a_recv.at[z, s],
+            device_id={"comp": z, "sub": s}, device_id_type=MESH).wait_recv()
 
     def pick(ty, i):
         return ty * 3 + (1 - 2 * ty) * i
@@ -609,8 +634,8 @@
         for n, j in enumerate(js):
             @pl.when(j < groups)
             def _():
-                for d in range(1, ncomp):
-                    chunk_copy(0, j, d).start()
+                for i in range(ncomp - 1):
+                    chunk_copy(0, j, i).start()
 
     straight = sub == lat
     code_copy(0).wait_recv()
@@ -653,31 +678,15 @@
 
     lax.fori_loop(0, kmax // FAR, far_body, 0)
 
-    def own_copy(h):
-        return pltpu.make_async_copy(
-            away_ref.at[h, me, pl.ds(0, groups)],
-            x_ref.at[h, 0, pl.ds(me * groups, groups), sub], o_sem.at[h])
-
-    def own_forward(h):
-        return pltpu.make_async_remote_copy(
-            src_ref=away_ref.at[h, me, pl.ds(0, groups)],
-            dst_ref=x_ref.at[h, 0, pl.ds(me * groups, groups), sub],
-            send_sem=f_send.at[h, 0], recv_sem=f_recv.at[h, 0],
+    own_copy = pltpu.make_async_copy(
+        away_ref.at[sub, me, pl.ds(0, groups)], x_ref.at[0, pl.ds(me * groups, groups), sub], o_sem)
+
+    def cross_copy():
+        return pltpu.make_async_remote_copy(
+            src_ref=away_ref.at[1 - sub, me, pl.ds(0, groups)],
+            dst_ref=x_ref.at[0, pl.ds(me * groups, groups), sub],
+            send_sem=a_send.at[0, ncomp - 1], recv_sem=a_recv.at[me, sub],
             device_id=partner, device_id_type=MESH)
-
-    def forward(h, d):
-        z = lax.rem(me + d, ncomp)
-        span = x_ref.at[h, 0, pl.ds(z * groups, groups), sub]
-        return pltpu.make_async_remote_copy(
-            src_ref=span, dst_ref=span, send_sem=f_send.at[h, d], recv_sem=f_recv.at[h, d],
-            device_id=partner, device_id_type=MESH)
-
-    def forward_wait(h, d):
-        z = lax.rem(me + d, ncomp)
-        span = x_ref.at[h, 0, pl.ds(z * groups, groups), 1 - sub]
-        pltpu.make_async_remote_copy(
-            src_ref=span, dst_ref=span, send_sem=f_send.at[h, d], recv_sem=f_recv.at[h, d],
-            device_id=partner, device_id_type=MESH).wait_recv()
 
     def prop_copy():
         return pltpu.make_async_remote_copy(
@@ -685,130 +694,96 @@
             dst_ref=pin_ref, send_sem=p_send, recv_sem=p_recv,
             device_id=partner, device_id_type=MESH)
 
-    for d in range(1, ncomp):
-        whole_copy(1, d).start()
-    for h in range(2):
-        own_copy(h).start()
-        own_forward(h).start()
+    own_copy.start()
+    cross_copy().start()
+    for i in range(ncomp - 1):
+        whole_copy(1, i).start()
     prop_copy().start()
-    load_w.wait()
-
-    def collect(h):
-        for d in range(1, ncomp):
-            whole_wait(h, lax.rem(me + d, ncomp))
-            forward(h, d).start()
-
-    def complete(h):
-        own_copy(h).wait()
-        for d in range(ncomp):
-            forward_wait(h, d)
-
-    first = sub * tiles * groups
-
-    def state_copy(h, step, m):
-        span = x_ref.at[h, step + 1, pl.ds(first + m * groups, groups)]
-        return pltpu.make_async_remote_copy(
-            src_ref=span, dst_ref=span, send_sem=e_send.at[h, step, m], recv_sem=e_recv.at[h, step, m],
-            device_id=partner, device_id_type=MESH)
-
-    def state_wait(h, step, m):
-        span = x_ref.at[h, step + 1, pl.ds((1 - sub) * tiles * groups + m * groups, groups)]
-        pltpu.make_async_remote_copy(
-            src_ref=span, dst_ref=span, send_sem=e_send.at[h, step, m], recv_sem=e_recv.at[h, step, m],
-            device_id=partner, device_id_type=MESH).wait_recv()
-
-    def home_copy(h, m):
-        to = sub * tiles + m
-        return to, pltpu.make_async_remote_copy(
-            src_ref=inc_ref.at[h, m], dst_ref=home_ref.at[me],
-            send_sem=b_send.at[h, m], recv_sem=b_recv.at[me],
-            device_id={"comp": to, "sub": h}, device_id_type=MESH)
-
-    def advance(h, step):
+
+    def home_copy(m):
+        return pltpu.make_async_remote_copy(
+            src_ref=inc_ref.at[m], dst_ref=home_ref.at[me],
+            send_sem=b_send.at[m], recv_sem=b_recv.at[me],
+            device_id={"comp": m}, device_id_type=MESH)
+
+    def advance(step):
         def one(i, carry):
-            m = lax.rem(i + 1 + me, tiles)
+            m = target(i)
             rows = pl.ds(pl.multiple_of(m * bins, 16), bins)
-            field = x_ref[h, step].reshape(total, lanes)
+            units = pl.ds(m * groups, groups)
+            field = x_ref[step % 2].reshape(total, lanes)
             driving = jnp.dot(w_ref[rows, :], field, preferred_element_type=F32)
             if step == 0:
-                now = x_ref[h, 0, pl.ds(first + m * groups, groups)].reshape(bins, lanes).astype(F32)
+                now = x_ref[0, units].reshape(bins, lanes).astype(F32)
+                start_ref[rows, :] = now
             else:
-                now = state_ref[h, rows, :]
+                now = state_ref[rows, :]
             now = now + STEP_SIZE * now * driving
             if step < SRC_STEPS - 1:
-                state_ref[h, rows, :] = now
-                x_ref[h, step + 1, pl.ds(first + m * groups, groups)] = now.astype(BF16).reshape(
-                    groups, 2, 16, lanes)
-                state_copy(h, step, m).start()
+                state_ref[rows, :] = now
+                x_ref[(step + 1) % 2, units] = now.astype(BF16).reshape(groups, 2, 16, lanes)
             else:
-                start = x_ref[h, 0, pl.ds(first + m * groups, groups)].reshape(bins, lanes).astype(F32)
-                gain = (now - start).astype(BF16)
-                inc_ref[h, m] = gain
-                to, copy = home_copy(h, m)
-                local = (to == me) & (sub == h)
-
-                @pl.when(jnp.logical_not(local))
+                inc_ref[m] = (now - start_ref[rows, :]).astype(BF16)
+
+                @pl.when(m != me)
                 def _():
-                    copy.start()
-
-                @pl.when(local)
-                def _():
-                    home_ref[me] = inc_ref[h, m]
+                    home_copy(m).start()
             return carry
 
-        if step > 0:
-            for m in range(tiles):
-                state_wait(h, step - 1, m)
-        lax.fori_loop(0, tiles, one, 0)
-
-    collect(0)
-    complete(0)
-    advance(0, 0)
-    advance(0, 1)
-    advance(0, 2)
-    collect(1)
-    advance(0, 3)
-    complete(1)
-    for step in range(SRC_STEPS):
-        advance(1, step)
+        lax.fori_loop(0, ncomp, one, 0)
 
     sea_wide = [jnp.broadcast_to(sea[:, r * NLON:(r + 1) * NLON], (16, NLON)) for r in range(2)]
-    prop_copy().wait_recv()
-
-    def restore(j, carry):
-        parts = [pout_ref[j, 2 * sub], pout_ref[j, 2 * sub + 1], pin_ref[j, 0], pin_ref[j, 1]]
+
+    def restore(g, carry):
+        js = [g * BACK + n for n in range(BACK)]
+        parts = [ref for j in js for ref in (
+            pout_ref[j, 2 * sub], pout_ref[j, 2 * sub + 1], pin_ref[j, 0], pin_ref[j, 1])]
         high, low = separate(jnp.concatenate(parts, axis=0))
         plain = (jnp.dot(high, perm_ref[1], preferred_element_type=F32)
                  + jnp.dot(low, perm_ref[1], preferred_element_type=F32))
-        for n in range(4):
-            p = sub if n < 2 else 1 - sub
-            rows = pl.ds(pl.multiple_of((2 * j + p) * 16, 16), 16)
+        for n in range(4 * BACK):
+            p = sub if n % 4 < 2 else 1 - sub
+            rows = pl.ds(pl.multiple_of((2 * js[n // 4] + p) * 16, 16), 16)
             r = n % 2
             out_ref[rows, r * NLON:(r + 1) * NLON] = sea_wide[r] * plain[n * 16:(n + 1) * 16, :]
         return carry
 
-    lax.fori_loop(0, groups, restore, 0)
-
-    mine_local = lax.div(me, tiles) == sub
-    for d in (0, 1, 3, 2):
-        z = lax.rem(me + d, ncomp)
+    def restore_all():
+        prop_copy().wait_recv()
+        lax.fori_loop(0, groups // BACK, restore, 0)
+
+    pl.when(sub == 1)(restore_all)
+    load_w.wait()
+    take_w().wait_recv()
+    own_copy.wait()
+    for z in range(ncomp):
+        for s in range(2):
+            @pl.when((z != me) | (s != sub))
+            def _():
+                whole_wait(z, s)
+
+    for step in range(SRC_STEPS):
+        advance(step)
+
+    pl.when(sub == 0)(restore_all)
+    for i in (3, 2, 1, 0):
+        z = target(i)
 
         def land():
             pltpu.make_async_remote_copy(
-                src_ref=inc_ref.at[0, 0], dst_ref=home_ref.at[z],
-                send_sem=b_send.at[0, 0], recv_sem=b_recv.at[z],
+                src_ref=inc_ref.at[z], dst_ref=home_ref.at[z],
+                send_sem=b_send.at[z], recv_sem=b_recv.at[z],
                 device_id={"comp": z}, device_id_type=MESH).wait_recv()
 
-        if d == 0:
-            pl.when(jnp.logical_not(mine_local))(land)
-        else:
+        if i < 3:
             land()
         r = lax.div(z, 2)
         half = lax.rem(z, 2)
         cols = pl.ds(pl.multiple_of(r * NLON, NLON), NLON)
         spread = perm_ref[1, pl.ds(pl.multiple_of(half * lanes, lanes), lanes), :]
         sea_row = jnp.where(r == 0, sea_wide[0][0:8], sea_wide[1][0:8])
-        back = jnp.dot(home_ref[z], spread, preferred_element_type=F32)
+        arrived = inc_ref[z] if i == 3 else home_ref[z]
+        back = jnp.dot(arrived, spread, preferred_element_type=F32)
         back = back.reshape(bins // 8, 8, NLON) * sea_row[None]
         out_ref[:, cols] = out_ref[:, cols] + back.reshape(bins, NLON)
 
@@ -825,19 +800,12 @@
 
     lax.fori_loop(0, kmax, halo_left, 0)
     prop_copy().wait_send()
-    for h in range(2):
-        own_forward(h).wait_send()
-        for d in range(1, ncomp):
-            whole_copy(h, d).wait_send()
-            forward(h, d).wait_send()
-        for m in range(tiles):
-            for step in range(SRC_STEPS - 1):
-                state_copy(h, step, m).wait_send()
-            to, copy = home_copy(h, m)
-
-            @pl.when(jnp.logical_not((to == me) & (sub == h)))
-            def _():
-                copy.wait_send()
+    cross_copy().wait_send()
+    give_w().wait_send()
+    for i in range(ncomp - 1):
+        for h in range(2):
+            whole_copy(h, i).wait_send()
+        home_copy(target(i)).wait_send()
 
 
 def write_kernel(src_ref, dst_ref, sems):
@@ -858,18 +826,20 @@
     kmax = (groups + 1) // 2
     lanes = NLON // 2
     total = bins * ncomp
-    tiles = ncomp // 2
     vmem = pl.BlockSpec(memory_space=pltpu.VMEM)
-    smem = pl.BlockSpec(memory_space=pltpu.SMEM)
-    hbm = pl.BlockSpec(memory_space=pl.ANY)
+    hbm = pl.BlockSpec(memory_space=pltpu.HBM)
     dma = pltpu.SemaphoreType.DMA
     result = pl.pallas_call(
         functools.partial(fast_kernel, ncomp),
         out_shape=pltpu.VMEM((bins, points), F32),
-        in_specs=[hbm, vmem, vmem, smem, smem, hbm],
+        in_specs=[hbm] * 6,
         out_specs=vmem,
         scratch_shapes=[
-            pltpu.VMEM((total // 2, total), BF16),
+            pltpu.VMEM((1, points), jnp.int32),
+            pltpu.VMEM((4, points), jnp.int32),
+            pltpu.SMEM(substeps.shape, jnp.int32),
+            pltpu.SMEM(courant.shape, F32),
+            pltpu.VMEM((total, total), BF16),
             pltpu.VMEM((2 * kmax, 4, 16, NLON), F32),
             pltpu.VMEM((2 * kmax, 2, 16, NLON), F32),
             pltpu.VMEM((kmax, 2, 2, 16, NLON), BF16),
@@ -881,18 +851,17 @@
             pltpu.VMEM((2 * kmax, 4, 16, NLON), F32),
             pltpu.VMEM((groups, 2, 16, NLON), F32),
             pltpu.VMEM((2, ncomp, 2 * kmax, 16, lanes), BF16),
-            pltpu.VMEM((2, SRC_STEPS, ncomp * groups, 2, 16, lanes), BF16),
-            pltpu.VMEM((2, total // 2, lanes), F32),
-            pltpu.VMEM((2, tiles, bins, lanes), BF16),
+            pltpu.VMEM((2, ncomp * groups, 2, 16, lanes), BF16),
+            pltpu.VMEM((total, lanes), F32),
+            pltpu.VMEM((total, lanes), F32),
             pltpu.VMEM((ncomp, bins, lanes), BF16),
-            dma((4,)), dma, dma((3,)), dma((3,)), dma, dma,
-            dma((kmax, 2)), dma((kmax, 2)), dma((2, ncomp)), dma((2, ncomp)), dma((2,)),
-            dma((2, ncomp)), dma((2, ncomp)), dma, dma,
-            dma((2, SRC_STEPS - 1, tiles)), dma((2, SRC_STEPS - 1, tiles)),
-            dma((2, tiles)), dma((ncomp,)),
+            pltpu.VMEM((ncomp, bins, lanes), BF16),
+            dma((4,)), dma((4,)), dma, dma((3,)), dma((3,)), dma, dma, dma, dma,
+            dma((kmax, 2)), dma((kmax, 2)), dma((2, ncomp)), dma((ncomp, 2)), dma, dma, dma,
+            dma((ncomp,)), dma((ncomp,)),
         ],
         compiler_params=pltpu.CompilerParams(
-            collective_id=1, has_side_effects=True, vmem_limit_bytes=48 * 1024 * 1024),
+            collective_id=1, has_side_effects=True, vmem_limit_bytes=60 * 1024 * 1024),
     )(spectrum.reshape(groups, 2, 16, points), sea_mask.reshape(1, points), neighbours, substeps, courant,
       source_operator)
     return pl.pallas_call(
@@ -910,7 +879,7 @@
 
     def per_device(spectrum, sea_mask, neighbours, substeps, courant, source_operator):
         bins, points = spectrum.shape
-        even = bins % 32 == 0 and (bins // 32 + 1) // 2 % NEAR == 0
+        even = bins % 32 == 0 and (bins // 32 + 1) // 2 % NEAR == 0 and bins // 32 % BACK == 0
         if nlat == 2 and ncomp == 4 and points == 2 * NLON and even:
             return fast_device(ncomp, spectrum, sea_mask, neighbours, substeps, courant, source_operator)
         size = 16 if bins % 16 == 0 else 8

time: 50.8 us -> 40.6 us (0.80)
  the two profiles are of different devices: /device:TPU:1 before, /device:TPU:13 now
where the time goes in v2:
time: 40.6 us; the launch traced here: 40.4 us
  Pallas kernels  40.4 us (100%)
    pallas_call x1, Pallas kernels, fast_device(): pl.pallas_call(functools.partial(fast_kernel, ncomp), out_shape=pltpu.VME...  39.4 us
    pallas_call x1, Pallas kernels, fast_device(): pl.pallas_call(write_kernel, out_shape=jax.ShapeDtypeStruct((bins, points...  0.97 us

profile of v2, /device:TPU:13, one launch (start us, length us, event | category | flops | bytes accessed | tf_op | source)
XLA Modules:
  0.0 40.4 jit_solution(1454093207414446400)
XLA Ops:
  0.0 39.4 %shard_map.64.src_ref = f32[480,512]{1,0:T(8,128)S(1)} custom-call(f32[15,2,16,512]{3,2,1,0:T(8,128)} %bitcast.2, s32[1,512]{1,0:T(1,128)} %bitcast.3, s32[4,512]{1,0:T(4,128)} %nb_hbm.1, s32[30]{0:T(128)} %steps_hbm.1, f32[30]{0:T(128)} %cour_hbm.1, bf16[960,1920]{1,0:T(8,128)(2,1)} %op_ref.1), custom_call_target="tpu_custom_call" | custom-call | tf_op jit(solution)/shard_map/pallas_call | solution.py:832
  39.4 1.0 %shard_map.65 = f32[480,512]{1,0:T(8,128)} custom-call(f32[480,512]{1,0:T(8,128)S(1)} %shard_map.64.src_ref), custom_call_target="tpu_custom_call" | custom-call | tf_op jit(solution)/shard_map/pallas_call | solution.py:867

commit v3 on v2

--- a/solution.py
+++ b/solution.py
@@ -369,7 +369,7 @@
 
 def fast_kernel(
     ncomp, spec_ref, mask_hbm, nb_hbm, steps_hbm, cour_hbm, op_ref,
-    out_ref, mask_ref, nb_ref, steps_ref, cour_ref, w_ref, full_ref, oth_ref, hsend_ref, halo_ref, raw_ref, code_ref, ang_ref, perm_ref,
+    out_ref, mask_ref, nb_ref, steps_ref, cour_ref, w_ref, full_ref, oth_ref, hsend_ref, halo_ref, code_ref, ang_ref, perm_ref,
     pout_ref, pin_ref, away_ref, x_ref, start_ref, state_ref, inc_ref, home_ref,
     l_sem, i_sem, w_sem, c_send, c_recv, r_send, r_recv, g_send, g_recv, h_send, h_recv,
     a_send, a_recv, o_sem, p_send, p_recv, b_send, b_recv,
@@ -386,9 +386,8 @@
     others = [partner, {"lat": 1 - lat}, {"lat": 1 - lat, "sub": 1 - sub}]
 
     small = [pltpu.make_async_copy(src, dst, i_sem.at[n]) for n, (src, dst) in enumerate((
-        (mask_hbm, mask_ref), (nb_hbm, nb_ref), (steps_hbm, steps_ref), (cour_hbm, cour_ref)))]
-    for load in small:
-        load.start()
+        (mask_hbm, mask_ref.at[lat, sub]), (nb_hbm, nb_ref.at[lat, sub]),
+        (steps_hbm, steps_ref), (cour_hbm, cour_ref)))]
     loads = []
     for r in range(2):
         cols = slice(r * NLON, (r + 1) * NLON)
@@ -396,7 +395,7 @@
             spec_ref.at[:, 1 - sub, :, cols], oth_ref.at[pl.ds(0, groups), r], l_sem.at[r]))
         loads.append(pltpu.make_async_copy(
             spec_ref.at[:, sub, :, cols], full_ref.at[pl.ds(0, groups), 2 * sub + r], l_sem.at[2 + r]))
-    for load in (loads[0], loads[2], loads[1], loads[3]):
+    for load in (small[0], *loads, *small[1:]):
         load.start()
     own_half = pl.ds(pl.multiple_of(sub * (total // 2), 16), total // 2)
     load_w = pltpu.make_async_copy(op_ref, w_ref.at[own_half], w_sem)
@@ -408,22 +407,6 @@
         peers += [{"comp": z}, {"comp": z, "sub": 1 - sub}]
     for peer in peers:
         pl.semaphore_signal(barrier, inc=1, device_id=peer, device_id_type=MESH)
-    load_w.start()
-    for load in small:
-        load.wait()
-
-    points = mask_ref.shape[1]
-    lane = lax.broadcasted_iota(jnp.int32, (1, points), 1)
-    column = lane & (NLON - 1)
-    sea = mask_ref[...].astype(F32)
-    west = (column - nb_ref[0:1, :]) & (NLON - 1)
-    east = (nb_ref[1:2, :] - column) & (NLON - 1)
-    moves = [((nb_ref[k:k + 1, :] - column + 1) & (NLON - 1)) - 1 for k in (2, 3)]
-    index = lax.broadcasted_iota(jnp.int32, (8, points), 0)
-    codes = jnp.zeros((8, points), F32)
-    for k, entry in enumerate([e.astype(F32) for e in (west, east, *moves)] + [sea]):
-        codes = jnp.where(index == k, jnp.broadcast_to(entry, (8, points)), codes)
-    raw_ref[lat, sub] = codes
 
     a = lax.broadcasted_iota(jnp.int32, (NLON, NLON), 0)
     b = lax.broadcasted_iota(jnp.int32, (NLON, NLON), 1)
@@ -441,6 +424,30 @@
         ang_ref[q, 0] = jnp.abs(jnp.cos(angle))
         ang_ref[q, 1] = jnp.abs(jnp.sin(angle))
 
+    def point_copies(n):
+        return [pltpu.make_async_remote_copy(
+            src_ref=ref.at[lat, sub], dst_ref=ref.at[lat, sub], send_sem=c_send.at[n, m],
+            recv_sem=c_recv.at[n, m], device_id=others[n], device_id_type=MESH)
+            for m, ref in enumerate((mask_ref, nb_ref))]
+
+    def raw_copies():
+        return [pltpu.make_async_remote_copy(
+            src_ref=spec_ref.at[:, 1 - sub, :, r * NLON:(r + 1) * NLON],
+            dst_ref=full_ref.at[pl.ds(0, groups), 2 * sub + r],
+            send_sem=r_send.at[r], recv_sem=r_recv.at[r], device_id=partner, device_id_type=MESH)
+            for r in range(2)]
+
+    def raw_waits():
+        for r in range(2):
+            pltpu.make_async_remote_copy(
+                src_ref=spec_ref.at[:, 1 - sub, :, r * NLON:(r + 1) * NLON],
+                dst_ref=full_ref.at[pl.ds(0, groups), 2 * (1 - sub) + r],
+                send_sem=r_send.at[r], recv_sem=r_recv.at[r],
+                device_id=partner, device_id_type=MESH).wait_recv()
+
+    small[0].wait()
+    small[1].wait()
+    sea = mask_ref[lat, sub].astype(F32)
     for load in loads:
         load.wait()
     sea_rows = [jnp.broadcast_to(sea[:, r * NLON:(r + 1) * NLON], (16, NLON)) for r in range(2)]
@@ -456,18 +463,6 @@
 
     lax.fori_loop(0, kmax, convert, 0)
     pl.semaphore_wait(barrier, len(peers))
-
-    def code_copy(n):
-        return pltpu.make_async_remote_copy(
-            src_ref=raw_ref.at[lat, sub], dst_ref=raw_ref.at[lat, sub], send_sem=c_send.at[n],
-            recv_sem=c_recv.at[n], device_id=others[n], device_id_type=MESH)
-
-    def raw_copy():
-        return pltpu.make_async_remote_copy(
-            src_ref=oth_ref.at[pl.ds(0, groups)],
-            dst_ref=full_ref.at[pl.ds(0, groups), pl.ds(2 * sub, 2)],
-            send_sem=r_send, recv_sem=r_recv, device_id=partner, device_id_type=MESH)
-
     def halo_copy(k, p):
         return pltpu.make_async_remote_copy(
             src_ref=hsend_ref.at[k, p], dst_ref=halo_ref.at[k, pl.ds(2 * sub, 2)],
@@ -480,11 +475,6 @@
             send_sem=h_send.at[k, s], recv_sem=h_recv.at[k, s],
             device_id={"lat": 1 - lat, "sub": s}, device_id_type=MESH).wait_recv()
 
-    code_copy(0).start()
-    raw_copy().start()
-    code_copy(1).start()
-    code_copy(2).start()
-
     def give_w():
         return pltpu.make_async_remote_copy(
             src_ref=op_ref, dst_ref=w_ref.at[own_half], send_sem=g_send, recv_sem=g_recv,
@@ -503,13 +493,33 @@
                 halo_copy(k, p).start()
         return carry
 
-    lax.fori_loop(0, kmax, send_halo, 0)
+    for copy in point_copies(0):
+        copy.start()
+    lax.fori_loop(0, FAR, send_halo, 0)
+    for copy in (*raw_copies(), *point_copies(1), *point_copies(2)):
+        copy.start()
+    lax.fori_loop(FAR, kmax, send_halo, 0)
+    load_w.start()
     give_w().start()
+    for load in small[2:]:
+        load.wait()
+
+    points = mask_ref.shape[-1]
+    lane = lax.broadcasted_iota(jnp.int32, (1, points), 1)
+    column = lane & (NLON - 1)
+    index = lax.broadcasted_iota(jnp.int32, (8, points), 0)
 
     def decode(chip):
         for s in range(2):
+            nb = nb_ref[chip, s]
+            west = (column - nb[0:1, :]) & (NLON - 1)
+            east = (nb[1:2, :] - column) & (NLON - 1)
+            moves = [((nb[k:k + 1, :] - column + 1) & (NLON - 1)) - 1 for k in (2, 3)]
+            codes = jnp.zeros((8, points), F32)
+            for k, entry in enumerate((west, east, *moves, mask_ref[chip, s])):
+                codes = jnp.where(index == k, jnp.broadcast_to(entry.astype(F32), (8, points)), codes)
             for r in range(2):
-                part = raw_ref[chip, s, :, r * NLON:(r + 1) * NLON].astype(BF16)
+                part = codes[:, r * NLON:(r + 1) * NLON].astype(BF16)
                 both = jnp.dot(part, perm_ref[0], preferred_element_type=F32)
                 for k in range(5):
                     code_ref[chip, 2 * s + r, k] = jnp.broadcast_to(both[k:k + 1, :], (8, NLON))
@@ -638,9 +648,10 @@
                     chunk_copy(0, j, i).start()
 
     straight = sub == lat
-    code_copy(0).wait_recv()
+    for copy in point_copies(0):
+        copy.wait_recv()
     decode(lat)
-    raw_copy().wait_recv()
+    raw_waits()
 
     def near_body(g, carry):
         ks = [g * NEAR + n for n in range(NEAR)]
@@ -655,8 +666,9 @@
         return carry
 
     lax.fori_loop(0, kmax // NEAR, near_body, 0)
-    code_copy(1).wait_recv()
-    code_copy(2).wait_recv()
+    for n in (1, 2):
+        for copy in point_copies(n):
+            copy.wait_recv()
     decode(1 - lat)
 
     def far_body(g, carry):
@@ -674,6 +686,12 @@
         @pl.when(jnp.logical_not(straight))
         def _():
             propagate(ks, True, True)
+
+        for k in ks:
+            @pl.when(n0 + 2 * k < groups)
+            def _():
+                for i in range(ncomp - 1):
+                    chunk_copy(1, n0 + 2 * k, i).start()
         return carry
 
     lax.fori_loop(0, kmax // FAR, far_body, 0)
@@ -696,8 +714,15 @@
 
     own_copy.start()
     cross_copy().start()
-    for i in range(ncomp - 1):
-        whole_copy(1, i).start()
+
+    def send_rest(k, carry):
+        @pl.when(f0 + 2 * k < groups)
+        def _():
+            for i in range(ncomp - 1):
+                chunk_copy(1, f0 + 2 * k, i).start()
+        return carry
+
+    lax.fori_loop(0, kmax, send_rest, 0)
     prop_copy().start()
 
     def home_copy(m):
@@ -706,28 +731,59 @@
             send_sem=b_send.at[m], recv_sem=b_recv.at[me],
             device_id={"comp": m}, device_id_type=MESH)
 
-    def advance(step):
+    early = (2 * bins) // 128 * 128
+    late = total - early
+
+    once = 1 + lax.div(me, ncomp)
+
+    def partial(start, span, use):
+        def one(i, carry):
+            rows = pl.ds(pl.multiple_of(i * total, 16), total)
+            field = x_ref[0, pl.ds(lax.div(start, 32), span // 32)].reshape(span, lanes)
+            cols = pl.ds(pl.multiple_of(start, 128), span)
+            use(rows, jnp.dot(w_ref[rows, cols], field, preferred_element_type=F32))
+            return carry
+
+        lax.fori_loop(0, once, one, 0)
+
+    def begin():
+        def use(rows, driving):
+            state_ref[rows, :] = driving
+
+        partial(side * late, early, use)
+
+    def first_step():
+        def use(rows, driving):
+            start = x_ref[0].reshape(total, lanes).astype(F32)
+            now = start + STEP_SIZE * start * (state_ref[rows, :] + driving)
+            start_ref[rows, :] = start
+            state_ref[rows, :] = now
+            x_ref[1] = now.astype(BF16).reshape(ncomp * groups, 2, 16, lanes)
+
+        partial((1 - side) * early, late, use)
+
+    def advance(step, carry):
+        field = x_ref[lax.rem(step, 2)].reshape(total, lanes)
+        driving = jnp.dot(w_ref[...], field, preferred_element_type=F32)
+        now = state_ref[...]
+        now = now + STEP_SIZE * now * driving
+        state_ref[...] = now
+        x_ref[lax.rem(step + 1, 2)] = now.astype(BF16).reshape(ncomp * groups, 2, 16, lanes)
+        return carry
+
+    def finish():
         def one(i, carry):
             m = target(i)
             rows = pl.ds(pl.multiple_of(m * bins, 16), bins)
-            units = pl.ds(m * groups, groups)
-            field = x_ref[step % 2].reshape(total, lanes)
+            field = x_ref[(SRC_STEPS - 1) % 2].reshape(total, lanes)
             driving = jnp.dot(w_ref[rows, :], field, preferred_element_type=F32)
-            if step == 0:
-                now = x_ref[0, units].reshape(bins, lanes).astype(F32)
-                start_ref[rows, :] = now
-            else:
-                now = state_ref[rows, :]
+            now = state_ref[rows, :]
             now = now + STEP_SIZE * now * driving
-            if step < SRC_STEPS - 1:
-                state_ref[rows, :] = now
-                x_ref[(step + 1) % 2, units] = now.astype(BF16).reshape(groups, 2, 16, lanes)
-            else:
-                inc_ref[m] = (now - start_ref[rows, :]).astype(BF16)
-
-                @pl.when(m != me)
-                def _():
-                    home_copy(m).start()
+            inc_ref[m] = (now - start_ref[rows, :]).astype(BF16)
+
+            @pl.when(m != me)
+            def _():
+                home_copy(m).start()
             return carry
 
         lax.fori_loop(0, ncomp, one, 0)
@@ -756,14 +812,16 @@
     load_w.wait()
     take_w().wait_recv()
     own_copy.wait()
-    for z in range(ncomp):
+    whole_wait(me, 1 - sub)
+    for s in range(2):
+        whole_wait(target(2), s)
+    begin()
+    for i in (1, 0):
         for s in range(2):
-            @pl.when((z != me) | (s != sub))
-            def _():
-                whole_wait(z, s)
-
-    for step in range(SRC_STEPS):
-        advance(step)
+            whole_wait(target(i), s)
+    first_step()
+    lax.fori_loop(1, SRC_STEPS - 1, advance, 0)
+    finish()
 
     pl.when(sub == 0)(restore_all)
     for i in (3, 2, 1, 0):
@@ -788,8 +846,10 @@
         out_ref[:, cols] = out_ref[:, cols] + back.reshape(bins, NLON)
 
     for n in range(3):
-        code_copy(n).wait_send()
-    raw_copy().wait_send()
+        for copy in point_copies(n):
+            copy.wait_send()
+    for copy in raw_copies():
+        copy.wait_send()
 
     def halo_left(k, carry):
         @pl.when(n0 + 2 * k < groups)
@@ -835,8 +895,8 @@
         in_specs=[hbm] * 6,
         out_specs=vmem,
         scratch_shapes=[
-            pltpu.VMEM((1, points), jnp.int32),
-            pltpu.VMEM((4, points), jnp.int32),
+            pltpu.VMEM((2, 2, 1, points), jnp.int32),
+            pltpu.VMEM((2, 2, 4, points), jnp.int32),
             pltpu.SMEM(substeps.shape, jnp.int32),
             pltpu.SMEM(courant.shape, F32),
             pltpu.VMEM((total, total), BF16),
@@ -844,7 +904,6 @@
             pltpu.VMEM((2 * kmax, 2, 16, NLON), F32),
             pltpu.VMEM((kmax, 2, 2, 16, NLON), BF16),
             pltpu.VMEM((kmax, 4, 16, NLON), BF16),
-            pltpu.VMEM((2, 2, 8, points), F32),
             pltpu.VMEM((2, 4, 5, 8, NLON), F32),
             pltpu.VMEM((2, 2, 16, lanes), F32),
             pltpu.VMEM((2, NLON, NLON), BF16),
@@ -856,7 +915,7 @@
             pltpu.VMEM((total, lanes), F32),
             pltpu.VMEM((ncomp, bins, lanes), BF16),
             pltpu.VMEM((ncomp, bins, lanes), BF16),
-            dma((4,)), dma((4,)), dma, dma((3,)), dma((3,)), dma, dma, dma, dma,
+            dma((4,)), dma((4,)), dma, dma((3, 2)), dma((3, 2)), dma((2,)), dma((2,)), dma, dma,
             dma((kmax, 2)), dma((kmax, 2)), dma((2, ncomp)), dma((ncomp, 2)), dma, dma, dma,
             dma((ncomp,)), dma((ncomp,)),
         ],

time: 40.6 us -> 38.2 us (0.941)
  the two profiles are of different devices: /device:TPU:13 before, /device:TPU:1 now
where the time goes in v3:
time: 38.2 us; the launch traced here: 38 us
  Pallas kernels  38 us (99%)
    pallas_call x1, Pallas kernels, fast_device(): pl.pallas_call(functools.partial(fast_kernel, ncomp), out_shape=pltpu.VME...  37 us
    pallas_call x1, Pallas kernels, fast_device(): pl.pallas_call(write_kernel, out_shape=jax.ShapeDtypeStruct((bins, points...  0.97 us

profile of v3, /device:TPU:1, one launch (start us, length us, event | category | flops | bytes accessed | tf_op | source)
XLA Modules:
  0.0 38.0 jit_solution(7873427845075989917)
XLA Ops:
  0.0 37.0 %shard_map.64.src_ref = f32[480,512]{1,0:T(8,128)S(1)} custom-call(f32[15,2,16,512]{3,2,1,0:T(8,128)} %bitcast.2, s32[1,512]{1,0:T(1,128)} %bitcast.3, s32[4,512]{1,0:T(4,128)} %nb_hbm.1, s32[30]{0:T(128)} %steps_hbm.1, f32[30]{0:T(128)} %cour_hbm.1, bf16[960,1920]{1,0:T(8,128)(2,1)} %op_ref.1), custom_call_target="tpu_custom_call" | custom-call | tf_op jit(solution)/shard_map/pallas_call | solution.py:892
  37.0 1.0 %shard_map.65 = f32[480,512]{1,0:T(8,128)} custom-call(f32[480,512]{1,0:T(8,128)S(1)} %shard_map.64.src_ref), custom_call_target="tpu_custom_call" | custom-call | tf_op jit(solution)/shard_map/pallas_call | solution.py:926

commit v4 on v3

--- a/solution.py
+++ b/solution.py
@@ -688,7 +688,7 @@
             propagate(ks, True, True)
 
         for k in ks:
-            @pl.when(n0 + 2 * k < groups)
+            @pl.when((n0 + 2 * k < groups) & (k < NEAR))
             def _():
                 for i in range(ncomp - 1):
                     chunk_copy(1, n0 + 2 * k, i).start()
@@ -722,7 +722,15 @@
                 chunk_copy(1, f0 + 2 * k, i).start()
         return carry
 
+    def send_near(k, carry):
+        @pl.when(n0 + 2 * k < groups)
+        def _():
+            for i in range(ncomp - 1):
+                chunk_copy(1, n0 + 2 * k, i).start()
+        return carry
+
     lax.fori_loop(0, kmax, send_rest, 0)
+    lax.fori_loop(NEAR, kmax, send_near, 0)
     prop_copy().start()
 
     def home_copy(m):

time: 38.2 us -> 37.4 us (0.979)
  Pallas kernels: 38 us -> 36.8 us
    pallas_call x1, Pallas kernels: 37 us -> 35.8 us  [fast_device(): pl.pallas_call(functools.partial(fast_kernel, ncomp), out_shape=pltpu.VME...]
where the time goes in v4:
time: 37.4 us; the launch traced here: 36.8 us
  Pallas kernels  36.8 us (98%)
    pallas_call x1, Pallas kernels, fast_device(): pl.pallas_call(functools.partial(fast_kernel, ncomp), out_shape=pltpu.VME...  35.8 us
    pallas_call x1, Pallas kernels, fast_device(): pl.pallas_call(write_kernel, out_shape=jax.ShapeDtypeStruct((bins, points...  0.97 us

profile of v4, /device:TPU:1, one launch (start us, length us, event | category | flops | bytes accessed | tf_op | source)
XLA Modules:
  0.0 36.8 jit_solution(10999508630617902136)
XLA Ops:
  0.0 35.8 %shard_map.64.src_ref = f32[480,512]{1,0:T(8,128)S(1)} custom-call(f32[15,2,16,512]{3,2,1,0:T(8,128)} %bitcast.2, s32[1,512]{1,0:T(1,128)} %bitcast.3, s32[4,512]{1,0:T(4,128)} %nb_hbm.1, s32[30]{0:T(128)} %steps_hbm.1, f32[30]{0:T(128)} %cour_hbm.1, bf16[960,1920]{1,0:T(8,128)(2,1)} %op_ref.1), custom_call_target="tpu_custom_call" | custom-call | tf_op jit(solution)/shard_map/pallas_call | solution.py:900
  35.8 1.0 %shard_map.65 = f32[480,512]{1,0:T(8,128)} custom-call(f32[480,512]{1,0:T(8,128)S(1)} %shard_map.64.src_ref), custom_call_target="tpu_custom_call" | custom-call | tf_op jit(solution)/shard_map/pallas_call | solution.py:934

commit v5 on v4

--- a/solution.py
+++ b/solution.py
@@ -22,6 +22,8 @@
 NEAR = 4
 FAR = 2
 BACK = 5
+AHEAD = 2
+PIECES = 2
 F32 = jnp.float32
 BF16 = jnp.bfloat16
 
@@ -372,7 +374,7 @@
     out_ref, mask_ref, nb_ref, steps_ref, cour_ref, w_ref, full_ref, oth_ref, hsend_ref, halo_ref, code_ref, ang_ref, perm_ref,
     pout_ref, pin_ref, away_ref, x_ref, start_ref, state_ref, inc_ref, home_ref,
     l_sem, i_sem, w_sem, c_send, c_recv, r_send, r_recv, g_send, g_recv, h_send, h_recv,
-    a_send, a_recv, o_sem, p_send, p_recv, b_send, b_recv,
+    a_send, a_recv, t_send, t_recv, o_sem, p_send, p_recv, b_send, b_recv,
 ):
     lat = lax.axis_index("lat")
     sub = lax.axis_index("sub")
@@ -495,10 +497,10 @@
 
     for copy in point_copies(0):
         copy.start()
-    lax.fori_loop(0, FAR, send_halo, 0)
+    lax.fori_loop(0, AHEAD, send_halo, 0)
     for copy in (*raw_copies(), *point_copies(1), *point_copies(2)):
         copy.start()
-    lax.fori_loop(FAR, kmax, send_halo, 0)
+    lax.fori_loop(AHEAD, kmax, send_halo, 0)
     load_w.start()
     give_w().start()
     for load in small[2:]:
@@ -533,7 +535,7 @@
     def chunk_copy(h, j, i):
         to = target(i)
         return pltpu.make_async_remote_copy(
-            src_ref=away_ref.at[h, to, j], dst_ref=x_ref.at[0, me * groups + j, sub],
+            src_ref=away_ref.at[h, to, j], dst_ref=x_ref.at[0, me * groups + j, sub, :, 0:lanes],
             send_sem=a_send.at[h, i], recv_sem=a_recv.at[me, sub],
             device_id={"comp": to, "sub": h}, device_id_type=MESH)
 
@@ -541,14 +543,14 @@
         to = target(i)
         return pltpu.make_async_remote_copy(
             src_ref=away_ref.at[h, to, pl.ds(0, groups)],
-            dst_ref=x_ref.at[0, pl.ds(me * groups, groups), sub],
+            dst_ref=x_ref.at[0, pl.ds(me * groups, groups), sub, :, 0:lanes],
             send_sem=a_send.at[h, i], recv_sem=a_recv.at[me, sub],
             device_id={"comp": to, "sub": h}, device_id_type=MESH)
 
     def whole_wait(z, s):
         pltpu.make_async_remote_copy(
             src_ref=away_ref.at[0, z, pl.ds(0, groups)],
-            dst_ref=x_ref.at[0, pl.ds(z * groups, groups), s],
+            dst_ref=x_ref.at[0, pl.ds(z * groups, groups), s, :, 0:lanes],
             send_sem=a_send.at[0, 0], recv_sem=a_recv.at[z, s],
             device_id={"comp": z, "sub": s}, device_id_type=MESH).wait_recv()
 
@@ -697,12 +699,12 @@
     lax.fori_loop(0, kmax // FAR, far_body, 0)
 
     own_copy = pltpu.make_async_copy(
-        away_ref.at[sub, me, pl.ds(0, groups)], x_ref.at[0, pl.ds(me * groups, groups), sub], o_sem)
+        away_ref.at[sub, me, pl.ds(0, groups)], x_ref.at[0, pl.ds(me * groups, groups), sub, :, 0:lanes], o_sem.at[0])
 
     def cross_copy():
         return pltpu.make_async_remote_copy(
             src_ref=away_ref.at[1 - sub, me, pl.ds(0, groups)],
-            dst_ref=x_ref.at[0, pl.ds(me * groups, groups), sub],
+            dst_ref=x_ref.at[0, pl.ds(me * groups, groups), sub, :, 0:lanes],
             send_sem=a_send.at[0, ncomp - 1], recv_sem=a_recv.at[me, sub],
             device_id=partner, device_id_type=MESH)
 
@@ -731,70 +733,150 @@
 
     lax.fori_loop(0, kmax, send_rest, 0)
     lax.fori_loop(NEAR, kmax, send_near, 0)
+
+    wide = (sub == 1) & (lax.div(me + 1, 2) == 1)
+
+    def twin_copy(block, to):
+        return pltpu.make_async_remote_copy(
+            src_ref=away_ref.at[1, block, pl.ds(0, groups)],
+            dst_ref=x_ref.at[0, pl.ds(me * groups, groups), sub, :, lanes:2 * lanes],
+            send_sem=t_send.at[block], recv_sem=t_recv.at[me, sub],
+            device_id={"comp": to, "sub": 1}, device_id_type=MESH)
+
+    def twin_local(block):
+        return pltpu.make_async_copy(
+            away_ref.at[1, block, pl.ds(0, groups)],
+            x_ref.at[0, pl.ds(me * groups, groups), sub, :, lanes:2 * lanes], o_sem.at[1])
+
+    def twin_wait(z, s):
+        pltpu.make_async_remote_copy(
+            src_ref=away_ref.at[1, 0, pl.ds(0, groups)],
+            dst_ref=x_ref.at[0, pl.ds(z * groups, groups), s, :, lanes:2 * lanes],
+            send_sem=t_send.at[0], recv_sem=t_recv.at[z, s],
+            device_id={"comp": z, "sub": s}, device_id_type=MESH).wait_recv()
+
+    def twin_here(to):
+        return (me == to) & (sub == 1)
+
+    for block, to in ((1, 2), (2, 1)):
+        @pl.when(jnp.logical_not(twin_here(to)))
+        def _():
+            twin_copy(block, to).start()
+
+        @pl.when(twin_here(to))
+        def _():
+            twin_local(block).start()
     prop_copy().start()
 
-    def home_copy(m):
-        return pltpu.make_async_remote_copy(
-            src_ref=inc_ref.at[m], dst_ref=home_ref.at[me],
-            send_sem=b_send.at[m], recv_sem=b_recv.at[me],
-            device_id={"comp": m}, device_id_type=MESH)
+    piece = bins // PIECES
+
+    def home_copy(source, block, to, start, size):
+        span = pl.ds(pl.multiple_of(start, 16), size)
+        return pltpu.make_async_remote_copy(
+            src_ref=inc_ref.at[source, span], dst_ref=home_ref.at[block, span],
+            send_sem=b_send.at[source], recv_sem=b_recv.at[block],
+            device_id={"comp": to}, device_id_type=MESH)
 
     early = (2 * bins) // 128 * 128
     late = total - early
 
     once = 1 + lax.div(me, ncomp)
 
-    def partial(start, span, use):
-        def one(i, carry):
-            rows = pl.ds(pl.multiple_of(i * total, 16), total)
-            field = x_ref[0, pl.ds(lax.div(start, 32), span // 32)].reshape(span, lanes)
-            cols = pl.ds(pl.multiple_of(start, 128), span)
-            use(rows, jnp.dot(w_ref[rows, cols], field, preferred_element_type=F32))
+    def integrate(width):
+        def partial(start, span, use):
+            def one(i, carry):
+                rows = pl.ds(pl.multiple_of(i * total, 16), total)
+                field = x_ref[0, pl.ds(lax.div(start, 32), span // 32), :, :, 0:width].reshape(span, width)
+                cols = pl.ds(pl.multiple_of(start, 128), span)
+                use(rows, jnp.dot(w_ref[rows, cols], field, preferred_element_type=F32))
+                return carry
+
+            lax.fori_loop(0, once, one, 0)
+
+        def begin(rows, driving):
+            state_ref[rows, 0:width] = driving
+
+        def first_step(rows, driving):
+            start = x_ref[0, :, :, :, 0:width].reshape(total, width).astype(F32)
+            now = start + STEP_SIZE * start * (state_ref[rows, 0:width] + driving)
+            start_ref[rows, 0:width] = start
+            state_ref[rows, 0:width] = now
+            x_ref[1, :, :, :, 0:width] = now.astype(BF16).reshape(ncomp * groups, 2, 16, width)
+
+        def advance(step, carry):
+            field = x_ref[lax.rem(step, 2), :, :, :, 0:width].reshape(total, width)
+            driving = jnp.dot(w_ref[...], field, preferred_element_type=F32)
+            now = state_ref[:, 0:width]
+            now = now + STEP_SIZE * now * driving
+            state_ref[:, 0:width] = now
+            x_ref[lax.rem(step + 1, 2), :, :, :, 0:width] = now.astype(BF16).reshape(
+                ncomp * groups, 2, 16, width)
             return carry
 
-        lax.fori_loop(0, once, one, 0)
-
-    def begin():
-        def use(rows, driving):
-            state_ref[rows, :] = driving
-
-        partial(side * late, early, use)
-
-    def first_step():
-        def use(rows, driving):
-            start = x_ref[0].reshape(total, lanes).astype(F32)
-            now = start + STEP_SIZE * start * (state_ref[rows, :] + driving)
-            start_ref[rows, :] = start
-            state_ref[rows, :] = now
-            x_ref[1] = now.astype(BF16).reshape(ncomp * groups, 2, 16, lanes)
-
-        partial((1 - side) * early, late, use)
-
-    def advance(step, carry):
-        field = x_ref[lax.rem(step, 2)].reshape(total, lanes)
-        driving = jnp.dot(w_ref[...], field, preferred_element_type=F32)
-        now = state_ref[...]
-        now = now + STEP_SIZE * now * driving
-        state_ref[...] = now
-        x_ref[lax.rem(step + 1, 2)] = now.astype(BF16).reshape(ncomp * groups, 2, 16, lanes)
-        return carry
-
-    def finish():
-        def one(i, carry):
-            m = target(i)
-            rows = pl.ds(pl.multiple_of(m * bins, 16), bins)
-            field = x_ref[(SRC_STEPS - 1) % 2].reshape(total, lanes)
+        def last(m, start):
+            rows = pl.ds(pl.multiple_of(m * bins + start, 16), piece)
+            field = x_ref[(SRC_STEPS - 1) % 2, :, :, :, 0:width].reshape(total, width)
             driving = jnp.dot(w_ref[rows, :], field, preferred_element_type=F32)
-            now = state_ref[rows, :]
+            now = state_ref[rows, 0:width]
             now = now + STEP_SIZE * now * driving
-            inc_ref[m] = (now - start_ref[rows, :]).astype(BF16)
+            return (now - start_ref[rows, 0:width]).astype(BF16)
+
+        def finish(n, carry):
+            m = target(lax.div(n, PIECES))
+            start = lax.rem(n, PIECES) * piece
+            span = pl.ds(pl.multiple_of(start, 16), piece)
+            gain = last(m, start)
+
+            @pl.when(m == me)
+            def _():
+                home_ref[me, span] = gain
 
             @pl.when(m != me)
             def _():
-                home_copy(m).start()
+                inc_ref[m, span] = gain
+                home_copy(m, me, m, start, piece).start()
             return carry
 
-        lax.fori_loop(0, ncomp, one, 0)
+        def finish_wide(n, carry):
+            m = target(lax.div(n, PIECES))
+            start = lax.rem(n, PIECES) * piece
+            span = pl.ds(pl.multiple_of(start, 16), piece)
+            gain = last(m, start)
+            blocks = ((me, gain[:, 0:lanes]), (3 - me, gain[:, lanes:2 * lanes]))
+
+            @pl.when(m == me)
+            def _():
+                for block, part in blocks:
+                    home_ref[block, span] = part
+
+            @pl.when(m != me)
+            def _():
+                for source, (block, part) in enumerate(blocks):
+                    inc_ref[source, span] = part
+                    home_copy(source, block, m, start, piece).start()
+            return carry
+
+        both = width > lanes
+        whole_wait(me, 1 - sub)
+        for s in range(2):
+            whole_wait(target(2), s)
+        if both:
+            twin_local(3 - me).wait()
+            twin_wait(me, 0)
+            for s in range(2):
+                twin_wait(target(2), s)
+        partial(side * late, early, begin)
+        for i in (1, 0):
+            for s in range(2):
+                whole_wait(target(i), s)
+                if both:
+                    twin_wait(target(i), s)
+        partial((1 - side) * early, late, first_step)
+        lax.fori_loop(1, SRC_STEPS - 1, advance, 0)
+        if both:
+            lax.fori_loop((ncomp - 2) * PIECES, ncomp * PIECES, finish_wide, 0)
+        else:
+            lax.fori_loop(0, ncomp * PIECES, finish, 0)
 
     sea_wide = [jnp.broadcast_to(sea[:, r * NLON:(r + 1) * NLON], (16, NLON)) for r in range(2)]
 
@@ -820,19 +902,16 @@
     load_w.wait()
     take_w().wait_recv()
     own_copy.wait()
-    whole_wait(me, 1 - sub)
-    for s in range(2):
-        whole_wait(target(2), s)
-    begin()
-    for i in (1, 0):
-        for s in range(2):
-            whole_wait(target(i), s)
-    first_step()
-    lax.fori_loop(1, SRC_STEPS - 1, advance, 0)
-    finish()
+    @pl.when(wide)
+    def _():
+        integrate(2 * lanes)
+
+    @pl.when(jnp.logical_not(wide))
+    def _():
+        integrate(lanes)
 
     pl.when(sub == 0)(restore_all)
-    for i in (3, 2, 1, 0):
+    for i in (3, 2, 0, 1):
         z = target(i)
 
         def land():
@@ -842,14 +921,13 @@
                 device_id={"comp": z}, device_id_type=MESH).wait_recv()
 
         if i < 3:
-            land()
+            pl.when(jnp.logical_not(wide & (z == 3 - me)))(land)
         r = lax.div(z, 2)
         half = lax.rem(z, 2)
         cols = pl.ds(pl.multiple_of(r * NLON, NLON), NLON)
         spread = perm_ref[1, pl.ds(pl.multiple_of(half * lanes, lanes), lanes), :]
         sea_row = jnp.where(r == 0, sea_wide[0][0:8], sea_wide[1][0:8])
-        arrived = inc_ref[z] if i == 3 else home_ref[z]
-        back = jnp.dot(arrived, spread, preferred_element_type=F32)
+        back = jnp.dot(home_ref[z], spread, preferred_element_type=F32)
         back = back.reshape(bins // 8, 8, NLON) * sea_row[None]
         out_ref[:, cols] = out_ref[:, cols] + back.reshape(bins, NLON)
 
@@ -873,7 +951,21 @@
     for i in range(ncomp - 1):
         for h in range(2):
             whole_copy(h, i).wait_send()
-        home_copy(target(i)).wait_send()
+
+        @pl.when(jnp.logical_not(wide))
+        def _():
+            m = target(i)
+            home_copy(m, me, m, 0, bins).wait_send()
+
+    @pl.when(wide)
+    def _():
+        for source, block in enumerate((me, 3 - me)):
+            home_copy(source, block, target(2), 0, bins).wait_send()
+
+    for block, to in ((1, 2), (2, 1)):
+        @pl.when(jnp.logical_not(twin_here(to)))
+        def _():
+            twin_copy(block, to).wait_send()
 
 
 def write_kernel(src_ref, dst_ref, sems):
@@ -918,13 +1010,14 @@
             pltpu.VMEM((2 * kmax, 4, 16, NLON), F32),
             pltpu.VMEM((groups, 2, 16, NLON), F32),
             pltpu.VMEM((2, ncomp, 2 * kmax, 16, lanes), BF16),
-            pltpu.VMEM((2, ncomp * groups, 2, 16, lanes), BF16),
-            pltpu.VMEM((total, lanes), F32),
-            pltpu.VMEM((total, lanes), F32),
+            pltpu.VMEM((2, ncomp * groups, 2, 16, 2 * lanes), BF16),
+            pltpu.VMEM((total, 2 * lanes), F32),
+            pltpu.VMEM((total, 2 * lanes), F32),
             pltpu.VMEM((ncomp, bins, lanes), BF16),
             pltpu.VMEM((ncomp, bins, lanes), BF16),
             dma((4,)), dma((4,)), dma, dma((3, 2)), dma((3, 2)), dma((2,)), dma((2,)), dma, dma,
-            dma((kmax, 2)), dma((kmax, 2)), dma((2, ncomp)), dma((ncomp, 2)), dma, dma, dma,
+            dma((kmax, 2)), dma((kmax, 2)), dma((2, ncomp)), dma((ncomp, 2)), dma((ncomp,)), dma((ncomp, 2)),
+            dma((2,)), dma, dma,
             dma((ncomp,)), dma((ncomp,)),
         ],
         compiler_params=pltpu.CompilerParams(

time: 37.4 us -> 36.7 us (0.981); the launches traced: 36.8 us -> 36.5 us
  no operation moved by 1% of the time
where the time goes in v5:
time: 36.7 us; the launch traced here: 36.5 us
  Pallas kernels  36.5 us (99%)
    pallas_call x1, Pallas kernels, fast_device(): pl.pallas_call(functools.partial(fast_kernel, ncomp), out_shape=pltpu.VME...  35.5 us
    pallas_call x1, Pallas kernels, fast_device(): pl.pallas_call(write_kernel, out_shape=jax.ShapeDtypeStruct((bins, points...  0.97 us

profile of v5, /device:TPU:1, one launch (start us, length us, event | category | flops | bytes accessed | tf_op | source)
XLA Modules:
  0.0 36.5 jit_solution(2875948558940752281)
XLA Ops:
  0.0 35.5 %shard_map.64.src_ref = f32[480,512]{1,0:T(8,128)S(1)} custom-call(f32[15,2,16,512]{3,2,1,0:T(8,128)} %bitcast.2, s32[1,512]{1,0:T(1,128)} %bitcast.3, s32[4,512]{1,0:T(4,128)} %nb_hbm.1, s32[30]{0:T(128)} %steps_hbm.1, f32[30]{0:T(128)} %cour_hbm.1, bf16[960,1920]{1,0:T(8,128)(2,1)} %op_ref.1), custom_call_target="tpu_custom_call" | custom-call | tf_op jit(solution)/shard_map/pallas_call | solution.py:992
  35.6 1.0 %shard_map.65 = f32[480,512]{1,0:T(8,128)} custom-call(f32[480,512]{1,0:T(8,128)S(1)} %shard_map.64.src_ref), custom_call_target="tpu_custom_call" | custom-call | tf_op jit(solution)/shard_map/pallas_call | solution.py:1027

commit v6 on v5

--- a/solution.py
+++ b/solution.py
@@ -532,19 +532,17 @@
         near = me + 1 - 2 * lax.rem(me, 2)
         return jnp.where(i == 0, 3 - 3 * side, jnp.where(i == 1, 2 - side, jnp.where(i == 2, near, me)))
 
-    def chunk_copy(h, j, i):
-        to = target(i)
+    def chunk_copy(h, j, to):
         return pltpu.make_async_remote_copy(
             src_ref=away_ref.at[h, to, j], dst_ref=x_ref.at[0, me * groups + j, sub, :, 0:lanes],
-            send_sem=a_send.at[h, i], recv_sem=a_recv.at[me, sub],
+            send_sem=a_send.at[h, to], recv_sem=a_recv.at[me, sub],
             device_id={"comp": to, "sub": h}, device_id_type=MESH)
 
-    def whole_copy(h, i):
-        to = target(i)
+    def whole_copy(h, to):
         return pltpu.make_async_remote_copy(
             src_ref=away_ref.at[h, to, pl.ds(0, groups)],
             dst_ref=x_ref.at[0, pl.ds(me * groups, groups), sub, :, 0:lanes],
-            send_sem=a_send.at[h, i], recv_sem=a_recv.at[me, sub],
+            send_sem=a_send.at[h, to], recv_sem=a_recv.at[me, sub],
             device_id={"comp": to, "sub": h}, device_id_type=MESH)
 
     def whole_wait(z, s):
@@ -647,7 +645,7 @@
             @pl.when(j < groups)
             def _():
                 for i in range(ncomp - 1):
-                    chunk_copy(0, j, i).start()
+                    chunk_copy(0, j, target(i)).start()
 
     straight = sub == lat
     for copy in point_copies(0):
@@ -672,6 +670,9 @@
         for copy in point_copies(n):
             copy.wait_recv()
     decode(1 - lat)
+
+    eager = 3 - 2 * side
+    patient = 2 - 2 * side
 
     def far_body(g, carry):
         ks = [g * FAR + n for n in range(FAR)]
@@ -690,10 +691,9 @@
             propagate(ks, True, True)
 
         for k in ks:
-            @pl.when((n0 + 2 * k < groups) & (k < NEAR))
+            @pl.when(n0 + 2 * k < groups)
             def _():
-                for i in range(ncomp - 1):
-                    chunk_copy(1, n0 + 2 * k, i).start()
+                chunk_copy(1, n0 + 2 * k, eager).start()
         return carry
 
     lax.fori_loop(0, kmax // FAR, far_body, 0)
@@ -705,7 +705,7 @@
         return pltpu.make_async_remote_copy(
             src_ref=away_ref.at[1 - sub, me, pl.ds(0, groups)],
             dst_ref=x_ref.at[0, pl.ds(me * groups, groups), sub, :, 0:lanes],
-            send_sem=a_send.at[0, ncomp - 1], recv_sem=a_recv.at[me, sub],
+            send_sem=a_send.at[0, me], recv_sem=a_recv.at[me, sub],
             device_id=partner, device_id_type=MESH)
 
     def prop_copy():
@@ -720,19 +720,10 @@
     def send_rest(k, carry):
         @pl.when(f0 + 2 * k < groups)
         def _():
-            for i in range(ncomp - 1):
-                chunk_copy(1, f0 + 2 * k, i).start()
+            chunk_copy(1, f0 + 2 * k, eager).start()
         return carry
 
-    def send_near(k, carry):
-        @pl.when(n0 + 2 * k < groups)
-        def _():
-            for i in range(ncomp - 1):
-                chunk_copy(1, n0 + 2 * k, i).start()
-        return carry
-
     lax.fori_loop(0, kmax, send_rest, 0)
-    lax.fori_loop(NEAR, kmax, send_near, 0)
 
     wide = (sub == 1) & (lax.div(me + 1, 2) == 1)
 
@@ -758,7 +749,7 @@
     def twin_here(to):
         return (me == to) & (sub == 1)
 
-    for block, to in ((1, 2), (2, 1)):
+    def send_twin(block, to):
         @pl.when(jnp.logical_not(twin_here(to)))
         def _():
             twin_copy(block, to).start()
@@ -766,6 +757,11 @@
         @pl.when(twin_here(to))
         def _():
             twin_local(block).start()
+
+    send_twin(2, 1)
+    whole_copy(1, target(2)).start()
+    whole_copy(1, patient).start()
+    send_twin(1, 2)
     prop_copy().start()
 
     piece = bins // PIECES
@@ -950,7 +946,7 @@
     give_w().wait_send()
     for i in range(ncomp - 1):
         for h in range(2):
-            whole_copy(h, i).wait_send()
+            whole_copy(h, target(i)).wait_send()
 
         @pl.when(jnp.logical_not(wide))
         def _():

time: 36.7 us -> 36.2 us (0.986)
  Pallas kernels: 36.5 us -> 36.1 us
    pallas_call x1, Pallas kernels: 35.5 us -> 35.1 us  [fast_device(): pl.pallas_call(functools.partial(fast_kernel, ncomp), out_shape=pltpu.VME...]
where the time goes in v6:
time: 36.2 us; the launch traced here: 36.1 us
  Pallas kernels  36.1 us (100%)
    pallas_call x1, Pallas kernels, fast_device(): pl.pallas_call(functools.partial(fast_kernel, ncomp), out_shape=pltpu.VME...  35.1 us
    pallas_call x1, Pallas kernels, fast_device(): pl.pallas_call(write_kernel, out_shape=jax.ShapeDtypeStruct((bins, points...  0.97 us

profile of v6, /device:TPU:1, one launch (start us, length us, event | category | flops | bytes accessed | tf_op | source)
XLA Modules:
  0.0 36.1 jit_solution(6544366321257985937)
XLA Ops:
  0.0 35.1 %shard_map.64.src_ref = f32[480,512]{1,0:T(8,128)S(1)} custom-call(f32[15,2,16,512]{3,2,1,0:T(8,128)} %bitcast.2, s32[1,512]{1,0:T(1,128)} %bitcast.3, s32[4,512]{1,0:T(4,128)} %nb_hbm.1, s32[30]{0:T(128)} %steps_hbm.1, f32[30]{0:T(128)} %cour_hbm.1, bf16[960,1920]{1,0:T(8,128)(2,1)} %op_ref.1), custom_call_target="tpu_custom_call" | custom-call | tf_op jit(solution)/shard_map/pallas_call | solution.py:988
  35.1 1.0 %shard_map.65 = f32[480,512]{1,0:T(8,128)} custom-call(f32[480,512]{1,0:T(8,128)S(1)} %shard_map.64.src_ref), custom_call_target="tpu_custom_call" | custom-call | tf_op jit(solution)/shard_map/pallas_call | solution.py:1023

commit v7 on v6

--- a/solution.py
+++ b/solution.py
@@ -531,6 +531,10 @@
     def target(i):
         near = me + 1 - 2 * lax.rem(me, 2)
         return jnp.where(i == 0, 3 - 3 * side, jnp.where(i == 1, 2 - side, jnp.where(i == 2, near, me)))
+
+    def outward(i):
+        k = lax.rem(i + 2, 3)
+        return target(jnp.where((side == 0) & (sub == 0) & (i < 3), k, i))
 
     def chunk_copy(h, j, to):
         return pltpu.make_async_remote_copy(
@@ -818,7 +822,7 @@
             return (now - start_ref[rows, 0:width]).astype(BF16)
 
         def finish(n, carry):
-            m = target(lax.div(n, PIECES))
+            m = outward(lax.div(n, PIECES))
             start = lax.rem(n, PIECES) * piece
             span = pl.ds(pl.multiple_of(start, 16), piece)
             gain = last(m, start)
@@ -907,7 +911,7 @@
         integrate(lanes)
 
     pl.when(sub == 0)(restore_all)
-    for i in (3, 2, 0, 1):
+    for i in (3, 0, 2, 1):
         z = target(i)
 
         def land():

time: 36.2 us -> 36 us (level)
  no operation moved by 1% of the time
where the time goes in v7:
time: 36 us; the launch traced here: 35.8 us
  Pallas kernels  35.8 us (99%)
    pallas_call x1, Pallas kernels, fast_device(): pl.pallas_call(functools.partial(fast_kernel, ncomp), out_shape=pltpu.VME...  34.8 us
    pallas_call x1, Pallas kernels, fast_device(): pl.pallas_call(write_kernel, out_shape=jax.ShapeDtypeStruct((bins, points...  0.97 us

profile of v7, /device:TPU:1, one launch (start us, length us, event | category | flops | bytes accessed | tf_op | source)
XLA Modules:
  0.0 35.8 jit_solution(11422607817673274276)
XLA Ops:
  0.0 34.8 %shard_map.64.src_ref = f32[480,512]{1,0:T(8,128)S(1)} custom-call(f32[15,2,16,512]{3,2,1,0:T(8,128)} %bitcast.2, s32[1,512]{1,0:T(1,128)} %bitcast.3, s32[4,512]{1,0:T(4,128)} %nb_hbm.1, s32[30]{0:T(128)} %steps_hbm.1, f32[30]{0:T(128)} %cour_hbm.1, bf16[960,1920]{1,0:T(8,128)(2,1)} %op_ref.1), custom_call_target="tpu_custom_call" | custom-call | tf_op jit(solution)/shard_map/pallas_call | solution.py:992
  34.8 1.0 %shard_map.65 = f32[480,512]{1,0:T(8,128)} custom-call(f32[480,512]{1,0:T(8,128)S(1)} %shard_map.64.src_ref), custom_call_target="tpu_custom_call" | custom-call | tf_op jit(solution)/shard_map/pallas_call | solution.py:1027

commit v8 on v7

--- a/solution.py
+++ b/solution.py
@@ -19,7 +19,7 @@
 HALF = ND // 2
 TILES = 4
 SLOTS = 8
-NEAR = 4
+NEAR = 2
 FAR = 2
 BACK = 5
 AHEAD = 2
@@ -432,20 +432,13 @@
             recv_sem=c_recv.at[n, m], device_id=others[n], device_id_type=MESH)
             for m, ref in enumerate((mask_ref, nb_ref))]
 
-    def raw_copies():
+    cut = 4 * NEAR
+
+    def raw_copies(core):
         return [pltpu.make_async_remote_copy(
-            src_ref=spec_ref.at[:, 1 - sub, :, r * NLON:(r + 1) * NLON],
-            dst_ref=full_ref.at[pl.ds(0, groups), 2 * sub + r],
-            send_sem=r_send.at[r], recv_sem=r_recv.at[r], device_id=partner, device_id_type=MESH)
-            for r in range(2)]
-
-    def raw_waits():
-        for r in range(2):
-            pltpu.make_async_remote_copy(
-                src_ref=spec_ref.at[:, 1 - sub, :, r * NLON:(r + 1) * NLON],
-                dst_ref=full_ref.at[pl.ds(0, groups), 2 * (1 - sub) + r],
-                send_sem=r_send.at[r], recv_sem=r_recv.at[r],
-                device_id=partner, device_id_type=MESH).wait_recv()
+            src_ref=oth_ref.at[pl.ds(a, n)], dst_ref=full_ref.at[pl.ds(a, n), pl.ds(2 * core, 2)],
+            send_sem=r_send.at[part], recv_sem=r_recv.at[part], device_id=partner, device_id_type=MESH)
+            for part, (a, n) in enumerate(((0, cut), (cut, groups - cut)))]
 
     small[0].wait()
     small[1].wait()
@@ -498,7 +491,7 @@
     for copy in point_copies(0):
         copy.start()
     lax.fori_loop(0, AHEAD, send_halo, 0)
-    for copy in (*raw_copies(), *point_copies(1), *point_copies(2)):
+    for copy in (*raw_copies(sub), *point_copies(1), *point_copies(2)):
         copy.start()
     lax.fori_loop(AHEAD, kmax, send_halo, 0)
     load_w.start()
@@ -655,9 +648,13 @@
     for copy in point_copies(0):
         copy.wait_recv()
     decode(lat)
-    raw_waits()
+    raw_copies(1 - sub)[0].wait_recv()
 
     def near_body(g, carry):
+        @pl.when(g == 2)
+        def _():
+            raw_copies(1 - sub)[1].wait_recv()
+
         ks = [g * NEAR + n for n in range(NEAR)]
 
         @pl.when(straight)
@@ -934,7 +931,7 @@
     for n in range(3):
         for copy in point_copies(n):
             copy.wait_send()
-    for copy in raw_copies():
+    for copy in raw_copies(sub):
         copy.wait_send()
 
     def halo_left(k, carry):

time: 36 us -> 36 us (level)
  no operation moved by 1% of the time
where the time goes in v8:
time: 36 us; the launch traced here: 35.8 us
  Pallas kernels  35.8 us (99%)
    pallas_call x1, Pallas kernels, fast_device(): pl.pallas_call(functools.partial(fast_kernel, ncomp), out_shape=pltpu.VME...  34.8 us
    pallas_call x1, Pallas kernels, fast_device(): pl.pallas_call(write_kernel, out_shape=jax.ShapeDtypeStruct((bins, points...  0.97 us

profile of v8, /device:TPU:1, one launch (start us, length us, event | category | flops | bytes accessed | tf_op | source)
XLA Modules:
  0.0 35.8 jit_solution(13146739699376661993)
XLA Ops:
  0.0 34.8 %shard_map.64.src_ref = f32[480,512]{1,0:T(8,128)S(1)} custom-call(f32[15,2,16,512]{3,2,1,0:T(8,128)} %bitcast.2, s32[1,512]{1,0:T(1,128)} %bitcast.3, s32[4,512]{1,0:T(4,128)} %nb_hbm.1, s32[30]{0:T(128)} %steps_hbm.1, f32[30]{0:T(128)} %cour_hbm.1, bf16[960,1920]{1,0:T(8,128)(2,1)} %op_ref.1), custom_call_target="tpu_custom_call" | custom-call | tf_op jit(solution)/shard_map/pallas_call | solution.py:989
  34.8 1.0 %shard_map.65 = f32[480,512]{1,0:T(8,128)} custom-call(f32[480,512]{1,0:T(8,128)S(1)} %shard_map.64.src_ref), custom_call_target="tpu_custom_call" | custom-call | tf_op jit(solution)/shard_map/pallas_call | solution.py:1024

commit v9 on v8

--- a/solution.py
+++ b/solution.py
@@ -760,8 +760,8 @@
             twin_local(block).start()
 
     send_twin(2, 1)
-    whole_copy(1, target(2)).start()
-    whole_copy(1, patient).start()
+    whole_copy(1, jnp.where(side == 0, target(2), patient)).start()
+    whole_copy(1, jnp.where(side == 0, patient, target(2))).start()
     send_twin(1, 2)
     prop_copy().start()
 

time: 36 us -> 36 us (level)
  no operation moved by 1% of the time
where the time goes in v9:
time: 36 us; the launch traced here: 35.8 us
  Pallas kernels  35.8 us (99%)
    pallas_call x1, Pallas kernels, fast_device(): pl.pallas_call(functools.partial(fast_kernel, ncomp), out_shape=pltpu.VME...  34.8 us
    pallas_call x1, Pallas kernels, fast_device(): pl.pallas_call(write_kernel, out_shape=jax.ShapeDtypeStruct((bins, points...  0.97 us

profile of v9, /device:TPU:1, one launch (start us, length us, event | category | flops | bytes accessed | tf_op | source)
XLA Modules:
  0.0 35.8 jit_solution(14481537568035734879)
XLA Ops:
  0.0 34.8 %shard_map.64.src_ref = f32[480,512]{1,0:T(8,128)S(1)} custom-call(f32[15,2,16,512]{3,2,1,0:T(8,128)} %bitcast.2, s32[1,512]{1,0:T(1,128)} %bitcast.3, s32[4,512]{1,0:T(4,128)} %nb_hbm.1, s32[30]{0:T(128)} %steps_hbm.1, f32[30]{0:T(128)} %cour_hbm.1, bf16[960,1920]{1,0:T(8,128)(2,1)} %op_ref.1), custom_call_target="tpu_custom_call" | custom-call | tf_op jit(solution)/shard_map/pallas_call | solution.py:989
  34.8 1.0 %shard_map.65 = f32[480,512]{1,0:T(8,128)} custom-call(f32[480,512]{1,0:T(8,128)S(1)} %shard_map.64.src_ref), custom_call_target="tpu_custom_call" | custom-call | tf_op jit(solution)/shard_map/pallas_call | solution.py:1024
